TPU v7x, 128 devices: a whole 4x4x4 slice. The times are simulated.
128 devices in a mesh: tau: 8 (over x, core), tile: 16 (over z, y).
Axes of the slice: x: 4, y: 4, z: 4, core: 2. Of those that a mesh axis runs over, the one named last changes fastest.
Arguments:
- occupied: bfloat16 [8, 2048, 128, 128], P('tau', 'tile'), may hold values from -6 to 6
- virtual: bfloat16 [8, 2048, 128, 128], P('tau', 'tile'), may hold values from -0.125 to 0.125
- cos_weights: float32 [4, 8], replicated, may hold values from -1 to 1
- pair_occ: int32 [3072, 16], P('tile'), may hold values from 0 to 127
- pair_virt: int32 [3072, 16], P('tile'), may hold values from 0 to 127
- partial_target_tile: int32 [3072], P('tile'), may hold values from 0 to 511, as said below
Outputs:
- spectrum: float32 [4, 512, 128, 128], P(None, 'tile', 'tau')
Inputs may be any that keep to these rules, and one draw needn't show every extreme that they name: `partial_target_tile`: within each aligned block of 192 entries, no owner (values d * 32 to (d + 1) * 32 - 1 for owner d) is named more than 24 times; one owner is named exactly 24 times in every block.
All inputs are finite; a program needn't handle non-finite values.
Results may differ from a plain program's by a relative error of at most 0.0003.
Values sent between devices are 32-bit elements; how exact they have to be, the bound alone decides.
A program may use at most 192 MiB of HBM per device.

v0:
```python
import functools
import math

import jax
import jax.numpy as jnp
from jax import lax
from jax.experimental import pallas as pl
from jax.experimental.pallas import tpu as pltpu
from jax.sharding import PartitionSpec as P

CHI_DEV = 32
UNIT = 4
BUDGET = 46 * 1024 * 1024
MESH = pl.DeviceIdType.MESH


def products_kernel(first, terms, chi_dev, occ_idx, virt_idx, target, occ, virt, out):
    owners, units, groups, each, rows, width = out.shape
    span = units * each
    count = target.shape[0]

    @pl.loop(0, owners)
    def _(d):
        out[d] = jnp.zeros(out.shape[1:], out.dtype)

    unroll = math.gcd(count, 4) if span == chi_dev else 1

    @pl.loop(0, count, unroll=unroll)
    def _(p):
        tile = target[p]
        owner = tile // chi_dev
        place = tile - owner * chi_dev - first

        def add():
            unit = place // each
            left = [occ[occ_idx[p * terms + j]] for j in range(terms)]
            right = [virt[virt_idx[p * terms + j]] for j in range(terms)]
            acc = jnp.dot(
                jnp.concatenate(left, axis=1),
                jnp.concatenate(right, axis=0),
                preferred_element_type=jnp.float32,
            )
            for g in range(groups):
                out[owner, unit, g, place - unit * each] += acc[g * rows : (g + 1) * rows]

        if span == chi_dev:
            add()
        else:
            pl.when((place >= 0) & (place < span))(add)


def products(occ, virt, occ_idx, virt_idx, target, first, span, each, owners, groups):
    terms = occ_idx.shape[1]
    size = occ.shape[1]
    smem = pl.BlockSpec(memory_space=pltpu.SMEM)
    vmem = pl.BlockSpec(memory_space=pltpu.VMEM)
    return pl.pallas_call(
        functools.partial(products_kernel, first, terms, CHI_DEV),
        out_shape=jax.ShapeDtypeStruct(
            (owners, span // each, groups, each, size // groups, size), jnp.float32
        ),
        in_specs=[smem, smem, smem, vmem, vmem],
        out_specs=vmem,
        compiler_params=pltpu.CompilerParams(vmem_limit_bytes=56 * 1024 * 1024),
        cost_estimate=pl.CostEstimate(
            flops=2 * target.shape[0] * terms * size**3 * span // CHI_DEV,
            bytes_accessed=occ.size * 4 + owners * span * size * size * 4,
            transcendentals=0,
        ),
    )(occ_idx.reshape(-1), virt_idx.reshape(-1), target, occ, virt)


def line_slots(n):
    if n == 1:
        return 0
    return 1 if n == 2 else 2 * (n - 1)


class Line:
    def __init__(self, n, place, device, own, slots, send_sem, recv_sem, hold=None):
        self.hold = hold
        self.n, self.place, self.device = n, place, device
        self.own, self.slots, self.send_sem, self.recv_sem = own, slots, send_sem, recv_sem

    def slot(self, right, d):
        if right:
            return d - 1
        return d if self.n == 2 else self.n - 1 + d

    def copy(self, right, u, d, src, back=False):
        s = self.slot(right, d)
        k = u * line_slots(self.n) + s
        return pltpu.make_async_remote_copy(
            src_ref=src,
            dst_ref=self.slots.at[s, u],
            send_sem=self.send_sem.at[k],
            recv_sem=self.recv_sem.at[k],
            device_id={"tile": self.device(1 if right != back else -1)},
            device_id_type=MESH,
        )

    def routes(self):
        for right in (True, False):
            for d in range(self.n - 1, 0, -1) if right else range(self.n - 1):
                yield right, d

    def launch(self, u):
        for right, d in self.routes():
            @pl.when(self.place == (0 if right else self.n - 1))
            def _():
                self.copy(right, u, d, self.own(d, u)).start()

    def merge(self, u):
        if self.n == 2:
            return
        for right, d in self.routes():
            inner = (self.place > 0) & (self.place < d) if right else (
                (self.place < self.n - 1) & (self.place > d))

            @pl.when(inner)
            def _():
                here = self.slots.at[self.slot(right, d), u]
                copy = self.copy(right, u, d, here)
                copy.wait_recv()
                own = self.own(d, u)
                if self.hold is not None:
                    buffer, sem = self.hold
                    fetch = pltpu.make_async_copy(own, buffer, sem)
                    fetch.start()
                    fetch.wait()
                    own = buffer
                here[...] += own[...]
                copy.start()

    def final(self, u, into):
        for right in (True, False):
            @pl.when(self.place > 0 if right else self.place < self.n - 1)
            def _():
                k = self.slot(right, self.place)
                here = self.slots.at[k, u]
                self.copy(right, u, self.place, here, back=True).wait_recv()
                into[...] += here[...]

    def drain(self, u):
        for right, d in self.routes():
            @pl.when(self.place < d if right else self.place > d)
            def _():
                self.copy(right, u, d, self.slots.at[self.slot(right, d), u]).wait_send()


def scatter_kernel(ny, nz, groups, weights, dense, out, mine, y_slots, z_slots, times,
                   load_sem, y_send, y_recv, z_send, z_recv, t_send, t_recv, hold, hold_sem,
                   both, z2_slots, y2_slots, both_sem, z2_send, z2_recv, y2_send, y2_recv):
    tau = lax.axis_index("tau")
    tile = lax.axis_index("tile")
    z, y = tile // ny, tile % ny
    units = mine.shape[0]
    last = units - 1
    each = mine.shape[3]
    freqs = out.shape[0]

    y_line = Line(ny, y, lambda step: tile + step, lambda d, u: dense.at[:, d, u],
                  y_slots, y_send, y_recv, (hold, hold_sem))
    z_line = Line(nz, z, lambda step: tile + step * ny, lambda d, u: mine.at[u, d],
                  z_slots, z_send, z_recv)

    z2_line = Line(nz, z, z_line.device, lambda d, u: both.at[d], z2_slots, z2_send, z2_recv)
    y2_line = Line(ny, y, y_line.device, lambda d, u: both.at[z, d], y2_slots, y2_send, y2_recv)

    barrier = pltpu.get_barrier_semaphore()
    for step in range(1, groups):
        pl.semaphore_signal(barrier, inc=1, device_id={"tau": (tau + step) % groups},
                            device_id_type=MESH)
    for step in range(1, ny):
        pl.semaphore_signal(barrier, inc=1, device_id={"tile": z * ny + (y + step) % ny},
                            device_id_type=MESH)
    for step in range(1, nz):
        pl.semaphore_signal(barrier, inc=1, device_id={"tile": (z + step) % nz * ny + y},
                            device_id_type=MESH)
    pl.semaphore_wait(barrier, groups - 1 + ny - 1 + nz - 1)

    def load(u):
        return pltpu.make_async_copy(dense.at[:, y, u], mine.at[u], load_sem.at[u])

    def swap(u, step):
        other = (tau + step) % groups
        return pltpu.make_async_remote_copy(
            src_ref=mine.at[u, z, other],
            dst_ref=times.at[u, tau],
            send_sem=t_send.at[u * groups + step],
            recv_sem=t_recv.at[u * groups + tau],
            device_id={"tau": other},
            device_id_type=MESH,
        )

    def arrived(u, source):
        return pltpu.make_async_remote_copy(
            src_ref=mine.at[u, z, 0],
            dst_ref=times.at[u, source],
            send_sem=t_send.at[u * groups],
            recv_sem=t_recv.at[u * groups + source],
            device_id={"tau": source},
            device_id_type=MESH,
        )

    whole = pltpu.make_async_copy(dense.at[:, :, last], both, both_sem)
    whole.start()

    @pl.loop(0, last)
    def _(u):
        y_line.launch(u)
        load(u).start()

    whole.wait()
    z2_line.launch(0)
    z2_line.merge(0)

    @pl.loop(0, units + 2)
    def _(t):
        @pl.when(t < last)
        def _():
            load(t).wait()
            y_line.merge(t)
            y_line.final(t, mine.at[t])
            z_line.launch(t)

        @pl.when(t == 0)
        def _():
            z2_line.final(0, both.at[z])
            y2_line.launch(0)

        @pl.when((t >= 1) & (t < units))
        def _():
            u = t - 1
            z_line.merge(u)
            z_line.final(u, mine.at[u, z])

        @pl.when(t == units)
        def _():
            y2_line.merge(0)
            mine[last, z] = both[z, y]
            y2_line.final(0, mine.at[last, z])

        @pl.when((t >= 1) & (t < units + 1))
        def _():
            u = t - 1
            for step in range(1, groups):
                swap(u, step).start()
            times[u, tau] = mine[u, z, tau]

        @pl.when(t >= 2)
        def _():
            u = t - 2
            for step in range(1, groups):
                arrived(u, (tau + step) % groups).wait_recv()
            for e in range(each):
                for k in range(freqs):
                    total = weights[k, 0] * times[u, 0, e]
                    for s in range(1, groups):
                        total += weights[k, s] * times[u, s, e]
                    out[k, u * each + e] = total

    z2_line.drain(0)
    y2_line.drain(0)

    @pl.loop(0, last)
    def _(u):
        y_line.drain(u)
        z_line.drain(u)

    @pl.loop(0, units)
    def _(u):
        for step in range(1, groups):
            swap(u, step).wait_send()


def scatter(dense, weights, ny, nz, groups):
    owners, units, _, each, rows, width = dense.shape
    freqs = weights.shape[0]
    block = (groups, each, rows, width)
    ys, zs = max(line_slots(ny), 1), max(line_slots(nz), 1)
    dma = pltpu.SemaphoreType.DMA
    return pl.pallas_call(
        functools.partial(scatter_kernel, ny, nz, groups),
        out_shape=jax.ShapeDtypeStruct((freqs, units * each, rows, width), jnp.float32),
        in_specs=[pl.BlockSpec(memory_space=pltpu.SMEM), pl.BlockSpec(memory_space=pl.ANY)],
        out_specs=pl.BlockSpec(memory_space=pltpu.VMEM),
        scratch_shapes=[
            pltpu.VMEM((units, nz) + block, jnp.float32),
            pltpu.VMEM((ys, units, nz) + block, jnp.float32),
            pltpu.VMEM((zs, units) + block, jnp.float32),
            pltpu.VMEM((units, groups, each, rows, width), jnp.float32),
            dma((units,)),
            dma((units * ys,)),
            dma((units * ys,)),
            dma((units * zs,)),
            dma((units * zs,)),
            dma((units * groups,)),
            dma((units * groups,)),
            pltpu.VMEM((nz,) + block if ny > 2 else (8, 128), jnp.float32),
            dma,
            pltpu.VMEM((nz, ny) + block, jnp.float32),
            pltpu.VMEM((zs, 1, ny) + block, jnp.float32),
            pltpu.VMEM((ys, 1) + block, jnp.float32),
            dma,
            dma((zs,)),
            dma((zs,)),
            dma((ys,)),
            dma((ys,)),
        ],
        compiler_params=pltpu.CompilerParams(
            collective_id=0, has_side_effects=True, vmem_limit_bytes=58 * 1024 * 1024),
    )(weights, dense.reshape((nz, ny) + dense.shape[1:]))


def body(occupied, virtual, cos_weights, pair_occ, pair_virt, partial_target_tile):
    owners = lax.axis_size("tile")
    groups = lax.axis_size("tau")
    size = occupied.shape[2]
    ny = 1
    while 2 * ny * 2 * ny <= owners:
        ny *= 2
    nz = owners // ny
    tile_bytes = 4 * size * size
    span = CHI_DEV
    while span > UNIT and span * tile_bytes * (
        nz * (1 + line_slots(ny)) + line_slots(nz) + 2
    ) > BUDGET:
        span //= 2
    results = []
    for q in range(CHI_DEV // span):
        dense = products(
            occupied[0], virtual[0], pair_occ, pair_virt, partial_target_tile,
            q * span, span, min(UNIT, span), owners, groups,
        )
        results.append(scatter(dense, cos_weights, ny, nz, groups))
    return results[0] if len(results) == 1 else jnp.concatenate(results, axis=1)


def solution(mesh):
    in_specs = (
        P("tau", "tile", None, None),
        P("tau", "tile", None, None),
        P(),
        P("tile", None),
        P("tile", None),
        P("tile"),
    )
    out_specs = P(None, "tile", "tau", None)
    return jax.shard_map(body, mesh=mesh, in_specs=in_specs, out_specs=out_specs, check_vma=False)
```

profile of v0, /device:TPU:1, one launch (start us, length us, event | category | flops | bytes accessed | tf_op | source)
XLA Modules:
  0.0 707.8 jit_solution(18390132588642822131)
XLA Ops:
  0.0 0.8 copy.7
  0.8 0.7 reshape.14.occ_idx
  1.5 0.8 copy.8
  2.3 0.7 reshape.15.virt_idx
  3.0 43.4 %shard_map.66 = f32[16,4,8,4,16,128]{5,4,3,2,1,0:T(8,128)} custom-call(s32[3072]{0:T(1024)} %reshape.14.occ_idx, s32[3072]{0:T(1024)} %reshape.15.virt_idx, s32[192]{0:T(256)} %target.3, bf16[128,128,128]{2,1,0:T(8,128)(2,1)} %bitcast.6, bf16[128,128,128]{2,1,0:T(8,128)(2,1)} %bitcast.8), custom_call_target="tpu_custom_call" | custom-call | flops 6442450944 | bytes 25165824 | tf_op jit(solution)/shard_map/pallas_call | solution.py:57
  46.4 309.0 %shard_map.67 = f32[4,16,16,128]{3,2,1,0:T(8,128)} custom-call(f32[4,8]{1,0:T(4,128)} %weights.3, f32[4,4,4,8,4,16,128]{6,5,4,3,2,1,0:T(8,128)} %bitcast.5), custom_call_target="tpu_custom_call" | custom-call | tf_op jit(solution)/shard_map/pallas_call | solution.py:283
  355.4 0.0 copy-start
  355.4 39.9 %shard_map.64 = f32[16,4,8,4,16,128]{5,4,3,2,1,0:T(8,128)} custom-call(s32[3072]{0:T(1024)} %reshape.14.occ_idx, s32[3072]{0:T(1024)} %reshape.15.virt_idx, s32[192]{0:T(256)} %target.3, bf16[128,128,128]{2,1,0:T(8,128)(2,1)} %bitcast.7, bf16[128,128,128]{2,1,0:T(8,128)(2,1)} %bitcast.9), custom_call_target="tpu_custom_call" | custom-call | flops 6442450944 | bytes 25165824 | tf_op jit(solution)/shard_map/pallas_call | solution.py:57
  395.4 310.3 %shard_map.65 = f32[4,16,16,128]{3,2,1,0:T(8,128)} custom-call(f32[4,8]{1,0:T(4,128)} %weights.3, f32[4,4,4,8,4,16,128]{6,5,4,3,2,1,0:T(8,128)} %bitcast.4), custom_call_target="tpu_custom_call" | custom-call | tf_op jit(solution)/shard_map/pallas_call | solution.py:283
  705.7 0.0 copy-done
  705.7 2.1 pad_maximum_fusion
Async XLA Ops:
  355.4 350.3 %copy-start = (f32[4,16,16,128]{3,2,1,0:T(8,128)S(1)}, f32[4,16,16,128]{3,2,1,0:T(8,128)}, u32[]{:S(2)}) copy-start(f32[4,16,16,128]{3,2,1,0:T(8,128)} %shard_map.67) | copy-start | bytes 1572868
where the time goes:
time: 705 us; the launch traced here: 708 us
  Pallas kernels  703 us (100%)
    pallas_call x2, Pallas kernels, scatter(): pl.pallas_call(functools.partial(scatter_kernel, ny, nz, groups), out_sha...  619 us
    pallas_call x2, Pallas kernels, products(): pl.pallas_call(functools.partial(products_kernel, first, terms, CHI_DEV),...  83.3 us

commit v1 on v0

v1 whole, which is shorter than its diff:
```python
import functools

import jax
import jax.numpy as jnp
from jax import lax
from jax.experimental import pallas as pl
from jax.experimental.pallas import tpu as pltpu
from jax.sharding import PartitionSpec as P

CHI_DEV = 32
CAP = 24
CHUNKS = 8
PBUFS = 3
YBUFS = 2
MESH = pl.DeviceIdType.MESH


def main_kernel(ny, nz, groups, terms,
                weights, occ_idx, virt_idx, part, keep, place, occ, virt, tv,
                out,
                pbuf, xrecv, freq, ybuf, yrecv, work, dense, zrecv, trecv, tbl_v, tbl,
                x_send, x_recv, y_send, y_recv, z_send, z_recv, t_send, t_recv, tbl_sem):
    tau = lax.axis_index("tau")
    tile = lax.axis_index("tile")
    z, y = tile // ny, tile % ny
    mine = (y, z)
    sizes = (ny, nz)
    freqs, _, rows, width = out.shape
    half = freqs // 2
    per = freq.shape[0]
    slots = yrecv.shape[3]
    each = slots // ny
    rounds = CHUNKS

    def peer(h, i):
        return {"tile": z * ny + i if h == 0 else i * ny + y}

    barrier = pltpu.get_barrier_semaphore()
    for step in range(1, groups):
        pl.semaphore_signal(barrier, inc=1, device_id={"tau": (tau + step) % groups},
                            device_id_type=MESH)
    for h in range(2):
        for step in range(1, sizes[h]):
            pl.semaphore_signal(barrier, inc=1, device_id=peer(h, (mine[h] + step) % sizes[h]),
                                device_id_type=MESH)
    pl.semaphore_wait(barrier, groups - 1 + ny - 1 + nz - 1)

    def meta(h, to, at):
        return pltpu.make_async_remote_copy(
            src_ref=tv.at[h, to], dst_ref=trecv.at[h, mine[h]],
            send_sem=t_send.at[h * 4 + to], recv_sem=t_recv.at[h * 4 + at],
            device_id=peer(h, to), device_id_type=MESH)

    def x_copy(c, to, at):
        return pltpu.make_async_remote_copy(
            src_ref=pbuf.at[c % PBUFS, to], dst_ref=xrecv.at[c, tau],
            send_sem=x_send.at[c * groups + to], recv_sem=x_recv.at[c * groups + at],
            device_id={"tau": to}, device_id_type=MESH)

    def x_arrival(c, source):
        return pltpu.make_async_remote_copy(
            src_ref=pbuf.at[c % PBUFS, 0], dst_ref=xrecv.at[c, source],
            send_sem=x_send.at[c * groups], recv_sem=x_recv.at[c * groups + source],
            device_id={"tau": source}, device_id_type=MESH)

    def y_copy(c, h, to, at):
        return pltpu.make_async_remote_copy(
            src_ref=ybuf.at[c % YBUFS, h, to], dst_ref=yrecv.at[c, h, mine[h]],
            send_sem=y_send.at[c * 8 + h * 4 + to], recv_sem=y_recv.at[c * 8 + h * 4 + at],
            device_id=peer(h, to), device_id_type=MESH)

    def y_arrival(c, h, source):
        return pltpu.make_async_remote_copy(
            src_ref=ybuf.at[c % YBUFS, h, 0], dst_ref=yrecv.at[c, h, source],
            send_sem=y_send.at[c * 8 + h * 4], recv_sem=y_recv.at[c * 8 + h * 4 + source],
            device_id=peer(h, source), device_id_type=MESH)

    def z_copy(h, to, at):
        return pltpu.make_async_remote_copy(
            src_ref=dense.at[h, to], dst_ref=zrecv.at[h, mine[1 - h]],
            send_sem=z_send.at[h * 4 + to], recv_sem=z_recv.at[h * 4 + at],
            device_id=peer(1 - h, to), device_id_type=MESH)

    def z_arrival(h, source):
        return pltpu.make_async_remote_copy(
            src_ref=dense.at[h, 0], dst_ref=zrecv.at[h, source],
            send_sem=z_send.at[h * 4], recv_sem=z_recv.at[h * 4 + source],
            device_id=peer(1 - h, source), device_id_type=MESH)

    def others(h):
        return [(mine[h] + step) % sizes[h] for step in range(1, sizes[h])]

    for h in range(2):
        for to in others(h):
            meta(h, to, mine[h]).start()
        trecv[h, mine[h]] = tv[h, mine[h]]
        for s in range(sizes[h]):
            work[h, s, slots] = jnp.zeros((half, rows, width), jnp.float32)
        for o in range(sizes[1 - h]):
            @pl.loop(0, CHI_DEV)
            def _(e):
                dense[h, o, e] = jnp.zeros((half, rows, width), jnp.float32)

    def compute(c):
        slot = c % PBUFS

        def one(i, last):
            n = c * per + i
            p = part[n]
            left = [occ[occ_idx[p * terms + j]] for j in range(terms)]
            right = [virt[virt_idx[p * terms + j]] for j in range(terms)]
            acc = jnp.dot(
                jnp.concatenate(left, axis=1),
                jnp.concatenate(right, axis=0),
                preferred_element_type=jnp.float32,
            )
            acc = acc + jnp.where(keep[n] != 0, last, 0.0)
            for g in range(groups):
                pbuf[slot, g, i] = acc[g * rows:(g + 1) * rows]
            return acc

        lax.fori_loop(0, per, one, jnp.zeros((rows * groups, width), jnp.float32))

    def transform(c):
        @pl.loop(0, per)
        def _(i):
            terms_in = [xrecv[c, s, i] for s in range(groups)]
            for k in range(freqs):
                total = weights[k, 0] * terms_in[0]
                for s in range(1, groups):
                    total += weights[k, s] * terms_in[s]
                freq[i, k] = total

        @pl.loop(0, nz)
        def _(dz):
            @pl.loop(0, ny)
            def _(dy):
                for m in range(each):
                    i = place[(c * ny * nz + dz * ny + dy) * each + m]
                    ybuf[c % YBUFS, 0, dy, dz * each + m] = freq[i, 0:half]
                    ybuf[c % YBUFS, 1, dz, dy * each + m] = freq[i, half:freqs]

    def tables():
        lane = lax.broadcasted_iota(jnp.int32, (CHUNKS, width), 1)
        for h in range(2):
            for s in others(h):
                meta(h, s, s).wait_recv()
            for s in range(sizes[h]):
                found = jnp.full((CHUNKS, width), slots, jnp.int32)
                for e in range(slots):
                    found = jnp.where(trecv[h, s, e] == lane, e, found)
                tbl_v[h, s] = found
        copy = pltpu.make_async_copy(tbl_v, tbl, tbl_sem)
        copy.start()
        copy.wait()

    def densify(c):
        for h in range(2):
            for s in range(sizes[h]):
                @pl.loop(0, slots)
                def _(e):
                    work[h, s, e] = yrecv[c, h, s, e]
        for h in range(2):
            @pl.loop(0, sizes[1 - h])
            def _(o):
                @pl.loop(0, CHI_DEV, unroll=2)
                def _(e):
                    total = dense[h, o, e]
                    for s in range(sizes[h]):
                        total += work[h, s, tbl[h, s, c, o * CHI_DEV + e]]
                    dense[h, o, e] = total

    @pl.loop(0, rounds + 2)
    def _(t):
        @pl.when(t < rounds)
        def _():
            @pl.when(t >= PBUFS)
            def _():
                for step in range(1, groups):
                    to = (tau + step) % groups
                    x_copy(t - PBUFS, to, tau).wait_send()
            compute(t)
            for step in range(1, groups):
                to = (tau + step) % groups
                x_copy(t, to, tau).start()

            @pl.loop(0, per)
            def _(i):
                xrecv[t, tau, i] = pbuf[t % PBUFS, tau, i]

        @pl.when((t >= 1) & (t < rounds + 1))
        def _():
            c = t - 1

            @pl.when(c >= YBUFS)
            def _():
                for h in range(2):
                    for to in others(h):
                        y_copy(c - YBUFS, h, to, mine[h]).wait_send()
            for step in range(1, groups):
                x_arrival(c, (tau + step) % groups).wait_recv()
            transform(c)
            for h in range(2):
                for to in others(h):
                    y_copy(c, h, to, mine[h]).start()

                @pl.loop(0, slots)
                def _(e):
                    yrecv[c, h, mine[h], e] = ybuf[c % YBUFS, h, mine[h], e]

        @pl.when(t == 2)
        def _():
            tables()

        @pl.when(t >= 2)
        def _():
            c = t - 2
            for h in range(2):
                for s in others(h):
                    y_arrival(c, h, s).wait_recv()
            densify(c)

    for h in range(2):
        for to in others(1 - h):
            z_copy(h, to, mine[1 - h]).start()
    for h in range(2):
        for s in others(1 - h):
            z_arrival(h, s).wait_recv()

        own = mine[1 - h]

        @pl.loop(0, CHI_DEV)
        def _(e):
            total = dense[h, own, e]
            for s in others(1 - h):
                total += zrecv[h, s, e]
            for k in range(half):
                out[h * half + k, e] = total[k]

    for h in range(2):
        for to in others(h):
            meta(h, to, mine[h]).wait_send()
        for to in others(1 - h):
            z_copy(h, to, mine[1 - h]).wait_send()

    @pl.loop(rounds - YBUFS, rounds)
    def _(c):
        for h in range(2):
            for to in others(h):
                y_copy(c, h, to, mine[h]).wait_send()

    @pl.loop(rounds - PBUFS, rounds)
    def _(c):
        for step in range(1, groups):
            x_copy(c, (tau + step) % groups, tau).wait_send()


def plan(target, owners, ny, nz):
    count = target.shape[0]
    per = count // CHUNKS
    each = CAP // CHUNKS
    index = jnp.arange(count, dtype=jnp.int32)
    key = target * 256 + index
    rank = jnp.sum((key[None, :] < key[:, None]).astype(jnp.int32), axis=1)
    ordered = jnp.sum(jnp.where(rank[:, None] == index[None, :], key[:, None], 0), axis=0)
    ordered = ordered.reshape(per, CHUNKS).T
    part = ordered & 255
    tile = ordered >> 8
    same = (tile[:, 1:] == tile[:, :-1]).astype(jnp.int32)
    none = jnp.zeros((CHUNKS, 1), jnp.int32)
    keep = jnp.concatenate([none, same], axis=1)
    last = 1 - jnp.concatenate([same, none], axis=1)
    owner = tile // CHI_DEV
    value = jnp.where(last != 0, tile - owner * CHI_DEV, -1)
    d = jnp.arange(owners, dtype=jnp.int32)
    start = jnp.sum((owner[:, None, :] < d[None, :, None]).astype(jnp.int32), axis=2)
    place = start[:, :, None] + jnp.arange(each, dtype=jnp.int32)
    within = jnp.arange(per, dtype=jnp.int32)
    hit = (place[..., None] == within) & (owner[:, None, None, :] == d[None, :, None, None])
    goal = jnp.sum(jnp.where(hit, value[:, None, None, :] + 1, 0), axis=3) - 1
    place = jnp.minimum(place, per - 1)
    goal = goal.reshape(CHUNKS, nz, ny, each)
    zs = jnp.arange(nz, dtype=jnp.int32)[None, :, None, None] * CHI_DEV
    ys = jnp.arange(ny, dtype=jnp.int32)[None, None, :, None] * CHI_DEV
    to_y = jnp.where(goal >= 0, goal + zs, -1).transpose(2, 1, 3, 0).reshape(ny, nz * each, CHUNKS)
    to_z = jnp.where(goal >= 0, goal + ys, -1).transpose(1, 2, 3, 0).reshape(nz, ny * each, CHUNKS)
    both = jnp.stack([to_y, to_z])
    both = jnp.broadcast_to(both[..., None], both.shape + (128,))
    return part.reshape(-1), keep.reshape(-1), place.reshape(-1), both


def body(occupied, virtual, cos_weights, pair_occ, pair_virt, partial_target_tile):
    owners = lax.axis_size("tile")
    groups = lax.axis_size("tau")
    size = occupied.shape[2]
    terms = pair_occ.shape[1]
    count = partial_target_tile.shape[0]
    freqs = cos_weights.shape[0]
    ny = 1
    while 2 * ny * 2 * ny <= owners:
        ny *= 2
    nz = owners // ny
    rows = size // groups
    per = count // CHUNKS
    slots = ny * (CAP // CHUNKS)
    half = freqs // 2
    part, keep, place, both = plan(partial_target_tile, owners, ny, nz)
    smem = pl.BlockSpec(memory_space=pltpu.SMEM)
    vmem = pl.BlockSpec(memory_space=pltpu.VMEM)
    dma = pltpu.SemaphoreType.DMA
    f32 = jnp.float32
    return pl.pallas_call(
        functools.partial(main_kernel, ny, nz, groups, terms),
        out_shape=jax.ShapeDtypeStruct((freqs, CHI_DEV, rows, size), f32),
        in_specs=[smem] * 6 + [vmem] * 3,
        out_specs=vmem,
        scratch_shapes=[
            pltpu.VMEM((PBUFS, groups, per, rows, size), f32),
            pltpu.VMEM((CHUNKS, groups, per, rows, size), f32),
            pltpu.VMEM((per, freqs, rows, size), f32),
            pltpu.VMEM((YBUFS, 2, ny, slots, half, rows, size), f32),
            pltpu.VMEM((CHUNKS, 2, ny, slots, half, rows, size), f32),
            pltpu.VMEM((2, ny, slots + 1, half, rows, size), f32),
            pltpu.VMEM((2, ny, CHI_DEV, half, rows, size), f32),
            pltpu.VMEM((2, ny, CHI_DEV, half, rows, size), f32),
            pltpu.VMEM((2, ny, slots, CHUNKS, size), jnp.int32),
            pltpu.VMEM((2, ny, CHUNKS, size), jnp.int32),
            pltpu.SMEM((2, ny, CHUNKS, size), jnp.int32),
            dma((CHUNKS * groups,)),
            dma((CHUNKS * groups,)),
            dma((CHUNKS * 8,)),
            dma((CHUNKS * 8,)),
            dma((8,)),
            dma((8,)),
            dma((8,)),
            dma((8,)),
            dma,
        ],
        compiler_params=pltpu.CompilerParams(
            collective_id=0, has_side_effects=True, vmem_limit_bytes=62 * 1024 * 1024),
    )(cos_weights, pair_occ.reshape(-1), pair_virt.reshape(-1), part, keep, place,
      occupied[0], virtual[0], both)


def solution(mesh):
    in_specs = (
        P("tau", "tile", None, None),
        P("tau", "tile", None, None),
        P(),
        P("tile", None),
        P("tile", None),
        P("tile"),
    )
    out_specs = P(None, "tile", "tau", None)
    return jax.shard_map(body, mesh=mesh, in_specs=in_specs, out_specs=out_specs, check_vma=False)
```

time: 705 us -> 209 us (0.30)
  Pallas kernels: 703 us -> 198 us
    pallas_call x4 -> x1, Pallas kernels: 703 us -> 198 us  [body(): pl.pallas_call(functools.partial(main_kernel, ny, nz, groups, terms), out...]
where the time goes in v1:
time: 209 us
  Pallas kernels  198 us (95%)
  local copies, waits for them, and re-layouts  8.83 us (4%)
  other arithmetic  2.18 us (1%)
    pallas_call x1, Pallas kernels, body(): pl.pallas_call(functools.partial(main_kernel, ny, nz, groups, terms), out...  198 us

profile of v1, /device:TPU:1, one launch (start us, length us, event | category | flops | bytes accessed | tf_op | source)
XLA Modules:
  0.0 208.9 jit_solution(13971206097676132598)
XLA Ops:
  0.0 0.7 iota_add_fusion.1
  0.7 0.2 convert_reduce_fusion
  0.9 0.1 select_reduce_fusion.1
  1.0 0.1 shift_right_arithmetic.14
  1.1 0.1 copy.41
  1.2 0.1 fusion.2
  1.3 0.1 select_add_fusion
  1.3 0.7 reshape.59.keep
  2.0 0.2 convert_reduce_fusion.1
  2.2 0.1 and.27
  2.4 0.7 reshape.58.part
  3.1 0.8 copy.38
  3.9 0.7 reshape.56.occ_idx
  4.6 0.8 copy.39
  5.4 0.7 reshape.57.virt_idx
  6.1 0.1 iota_add_fusion
  6.2 0.1 copy.42
  6.3 0.6 select_reduce_fusion
  6.9 0.8 min.12.place
  7.7 0.1 copy.44
  7.7 0.1 select_bitcast_fusion.1
  7.9 0.9 broadcast_in_dim.27.tv
  8.8 197.8 %shard_map.64 = f32[4,32,16,128]{3,2,1,0:T(8,128)} custom-call(f32[4,8]{1,0:T(4,128)} %weights.1, s32[3072]{0:T(1024)} %reshape.56.occ_idx, s32[3072]{0:T(1024)} %reshape.57.virt_idx, s32[192]{0:T(256)} %reshape.58.part, s32[192]{0:T(256)} %reshape.59.keep, s32[384]{0:T(512)} %min.12.place, bf16[128,128,128]{2,1,0:T(8,128)(2,1)} %bitcast.15, ...), custom_call_target="tpu_custom_call" | custom-call | tf_op jit(solution)/shard_map/pallas_call | solution.py:312
  206.6 2.3 %copy.50 = f32[4,32,16,128]{3,2,1,0:T(8,128)} copy(f32[4,32,16,128]{3,2,1,0:T(8,128)} %shard_map.64) | data formatting | bytes 2097152
  (9 shorter events, 0.1 us)

commit v2 on v1

v2 whole, which is shorter than its diff:
```python
import functools
import math

import jax
import jax.numpy as jnp
from jax import lax
from jax.experimental import pallas as pl
from jax.experimental.pallas import tpu as pltpu
from jax.sharding import PartitionSpec as P

CHI_DEV = 32
CAP = 24
CHUNKS = 8
PBUFS = 3
YBUFS = 2
RING = 4
LAG = 3
MESH = pl.DeviceIdType.MESH


def main_kernel(ny, nz, groups, terms,
                weights, occ_idx, virt_idx, part, keep, place, occ, virt, tv,
                out,
                early, late, timed, x_early, x_late, freq, ybuf, yrecv, work, dense, zrecv,
                final, back, trecv, tbl_v, tbl,
                e_send, e_recv, l_send, l_recv, y_send, y_recv, z_send, z_recv,
                b_send, b_recv, t_send, t_recv, tbl_sem):
    tau = lax.axis_index("tau")
    tile = lax.axis_index("tile")
    x, core = tau // 2, tau % 2
    nx = groups // 2
    z, y = tile // ny, tile % ny
    mine = (y, z)
    sizes = (ny, nz)
    freqs, _, rows, width = out.shape
    low = rows // 2
    half = freqs // 2
    per = freq.shape[0]
    slots = yrecv.shape[4]
    each = slots // ny
    rounds = CHUNKS

    def peer(h, i):
        return {"tile": z * ny + i if h == 0 else i * ny + y}

    def others(h):
        return [(mine[h] + step) % sizes[h] for step in range(1, sizes[h])]

    def times():
        return [(tau + step) % groups for step in range(1, groups)]

    barrier = pltpu.get_barrier_semaphore()
    for to in times():
        pl.semaphore_signal(barrier, inc=1, device_id={"tau": to}, device_id_type=MESH)
    for h in range(2):
        for to in others(h):
            pl.semaphore_signal(barrier, inc=1, device_id=peer(h, to), device_id_type=MESH)
    pl.semaphore_wait(barrier, groups - 1 + ny - 1 + nz - 1)

    def meta(h, to, at):
        return pltpu.make_async_remote_copy(
            src_ref=tv.at[h, to], dst_ref=trecv.at[h, mine[h]],
            send_sem=t_send.at[h * 4 + to], recv_sem=t_recv.at[h * 4 + at],
            device_id=peer(h, to), device_id_type=MESH)

    def early_copy(c, to, source):
        return pltpu.make_async_remote_copy(
            src_ref=early.at[c % PBUFS, to], dst_ref=x_early.at[c % RING, source],
            send_sem=e_send.at[c % PBUFS * groups + to],
            recv_sem=e_recv.at[c % RING * groups + source],
            device_id={"tau": to}, device_id_type=MESH)

    def late_copy(c, dest, source):
        return pltpu.make_async_remote_copy(
            src_ref=late.at[c, dest], dst_ref=x_late.at[c, source],
            send_sem=l_send.at[c * nx + dest],
            recv_sem=l_recv.at[c * groups + source],
            device_id={"tau": 2 * dest + 1}, device_id_type=MESH)

    def late_each(c, act):
        for step in range(nx):
            dest = (x + step) % nx
            if step == 0:
                @pl.when(core == 0)
                def _():
                    act(late_copy(c, dest, tau))
            else:
                act(late_copy(c, dest, tau))

    def y_copy(q, c, h, to, source):
        return pltpu.make_async_remote_copy(
            src_ref=ybuf.at[q, c % YBUFS, h, to], dst_ref=yrecv.at[q, c % RING, h, source],
            send_sem=y_send.at[((q * YBUFS + c % YBUFS) * 2 + h) * 4 + to],
            recv_sem=y_recv.at[((q * RING + c % RING) * 2 + h) * 4 + source],
            device_id=peer(h, to), device_id_type=MESH)

    def z_copy(q, h, to, source):
        return pltpu.make_async_remote_copy(
            src_ref=dense.at[q, h, to], dst_ref=zrecv.at[q, h, source],
            send_sem=z_send.at[(q * 2 + h) * 4 + to],
            recv_sem=z_recv.at[(q * 2 + h) * 4 + source],
            device_id=peer(1 - h, to), device_id_type=MESH)

    def back_copy(dest, source):
        return pltpu.make_async_remote_copy(
            src_ref=final.at[dest], dst_ref=back.at[source],
            send_sem=b_send.at[dest], recv_sem=b_recv.at[source],
            device_id={"tau": 2 * dest}, device_id_type=MESH)

    def back_each(act):
        for step in range(nx):
            dest = (x + step) % nx
            if step == 0:
                @pl.when(core == 1)
                def _():
                    act(back_copy(dest, tau))
            else:
                act(back_copy(dest, tau))

    for h in range(2):
        for to in others(h):
            meta(h, to, mine[h]).start()
        trecv[h, mine[h]] = tv[h, mine[h]]
        for s in range(sizes[h]):
            work[h, s * (slots + 1) + slots] = jnp.zeros((half, low, width), jnp.float32)

    @pl.loop(0, CHI_DEV)
    def _(e):
        for q in range(3):
            for h in range(2):
                for o in range(sizes[1 - h]):
                    dense[q, h, o, e] = jnp.zeros((half, low, width), jnp.float32)

    def compute(c):
        slot = c % PBUFS

        def one(i, last):
            n = c * per + i
            p = part[n]
            left = [occ[occ_idx[p * terms + j]] for j in range(terms)]
            right = [virt[virt_idx[p * terms + j]] for j in range(terms)]
            acc = jnp.dot(
                jnp.concatenate(left, axis=1),
                jnp.concatenate(right, axis=0),
                preferred_element_type=jnp.float32,
            )
            acc = acc + jnp.where(keep[n] != 0, last, 0.0)
            for g in range(groups):
                early[slot, g, i] = acc[g * rows:g * rows + low]
                upper = acc[g * rows + low:(g + 1) * rows]
                if g % 2 == 0:
                    timed[i, g // 2] = upper
                else:
                    late[c, g // 2, i] = upper
            return acc

        lax.fori_loop(0, per, one, jnp.zeros((rows * groups, width), jnp.float32),
                      unroll=math.gcd(per, 4))

    def transform(landed, at):
        @pl.loop(0, per, unroll=2)
        def _(i):
            values = [landed[at, s, i] for s in range(groups)]
            for k in range(freqs):
                total = weights[k, 0] * values[0]
                for s in range(1, groups):
                    total += weights[k, s] * values[s]
                freq[i, k] = total

    def send_y(q, c, values):
        @pl.when(c >= YBUFS)
        def _():
            for h in range(2):
                for to in others(h):
                    y_copy(q, c - YBUFS, h, to, mine[h]).wait_send()

        @pl.loop(0, nz)
        def _(dz):
            for dy in range(ny):
                for m in range(each):
                    i = place[(c * ny * nz + dz * ny + dy) * each + m]
                    ybuf[q, c % YBUFS, 0, dy, dz * each + m] = values[i, 0:half]
                    ybuf[q, c % YBUFS, 1, dz, dy * each + m] = values[i, half:freqs]

        for h in range(2):
            for to in others(h):
                y_copy(q, c, h, to, mine[h]).start()
            for e in range(slots):
                yrecv[q, c % RING, h, mine[h], e] = ybuf[q, c % YBUFS, h, mine[h], e]

    def tables():
        lane = lax.broadcasted_iota(jnp.int32, (CHUNKS, width), 1)
        for h in range(2):
            for s in others(h):
                meta(h, s, s).wait_recv()
            packed = jnp.zeros((CHUNKS, width), jnp.int32)
            for s in range(sizes[h]):
                found = jnp.full((CHUNKS, width), slots, jnp.int32)
                for e in range(slots):
                    found = jnp.where(trecv[h, s, e] == lane, e, found)
                packed = packed + (found + s * (slots + 1)) * (1 << (8 * s))
            tbl_v[h] = packed
        copy = pltpu.make_async_copy(tbl_v, tbl, tbl_sem)
        copy.start()
        copy.wait()

    def densify(q, c):
        for h in range(2):
            for s in others(h):
                y_copy(q, c, h, s, s).wait_recv()
            for s in range(sizes[h]):
                for e in range(slots):
                    work[h, s * (slots + 1) + e] = yrecv[q, c % RING, h, s, e]
        for h in range(2):
            @pl.loop(0, sizes[1 - h])
            def _(o):
                @pl.loop(0, CHI_DEV, unroll=8)
                def _(e):
                    packed = tbl[h, c, o * CHI_DEV + e]
                    total = dense[q, h, o, e]
                    for s in range(sizes[h]):
                        total += work[h, (packed >> (8 * s)) & 255]
                    dense[q, h, o, e] = total

    def send_z(q):
        for h in range(2):
            for to in others(1 - h):
                z_copy(q, h, to, mine[1 - h]).start()

    def finish(q, store):
        for h in range(2):
            for s in others(1 - h):
                z_copy(q, h, s, s).wait_recv()
            own = mine[1 - h]

            @pl.loop(0, CHI_DEV, unroll=4)
            def _(e):
                total = dense[q, h, own, e]
                for s in others(1 - h):
                    total += zrecv[q, h, s, e]
                for k in range(half):
                    store(h * half + k, e, total[k])

    def store_early(k, e, value):
        out[k, e, 0:low] = value

    def store_late(k, e, value):
        out[k, e, low:rows] = value

    def store_final(k, e, value):
        final[k, e] = value

    @pl.loop(0, rounds + LAG + 2)
    def _(t):
        @pl.when(t < rounds)
        def _():
            @pl.when(t >= PBUFS)
            def _():
                for to in times():
                    early_copy(t - PBUFS, to, tau).wait_send()
            compute(t)
            for to in times():
                early_copy(t, to, tau).start()

        @pl.when((t >= LAG) & (t < rounds + LAG))
        def _():
            late_each(t - LAG, lambda copy: copy.start())

        @pl.when(t < rounds)
        def _():
            send_y(2, t, timed)

            @pl.loop(0, per, unroll=4)
            def _(i):
                x_early[t % RING, tau, i] = early[t % PBUFS, tau, i]

        @pl.when((t >= 1) & (t < rounds + 1))
        def _():
            c = t - 1
            for s in times():
                early_copy(c, s, s).wait_recv()
            transform(x_early, c % RING)
            send_y(0, c, freq)

        @pl.when((t >= LAG + 1) & (t < rounds + LAG + 1) & (core == 1))
        def _():
            c = t - LAG - 1

            @pl.loop(0, per, unroll=4)
            def _(i):
                x_late[c, tau, i] = late[c, x, i]
            for s in times():
                late_copy(c, x, s).wait_recv()
            transform(x_late, c)
            send_y(1, c, freq)

        @pl.when(t == 1)
        def _():
            tables()

        @pl.when((t >= 1) & (t < rounds + 1))
        def _():
            densify(2, t - 1)

        @pl.when(t == rounds)
        def _():
            send_z(2)

        @pl.when((t >= 2) & (t < rounds + 2))
        def _():
            densify(0, t - 2)

        @pl.when(t == rounds + 1)
        def _():
            send_z(0)
            finish(2, store_final)
            back_each(lambda copy: copy.start())

        @pl.when((t >= LAG + 2) & (core == 1))
        def _():
            densify(1, t - LAG - 2)

    @pl.when(core == 1)
    def _():
        send_z(1)

    finish(0, store_early)

    @pl.when(core == 1)
    def _():
        finish(1, store_late)

    @pl.when(core == 0)
    def _():
        @pl.loop(0, CHI_DEV, unroll=4)
        def _(e):
            back[tau, e] = final[x, e]
        for s in times():
            back_copy(x, s).wait_recv()

        @pl.loop(0, CHI_DEV, unroll=2)
        def _(e):
            values = [back[s, e] for s in range(groups)]
            for k in range(freqs):
                total = weights[k, 0] * values[0]
                for s in range(1, groups):
                    total += weights[k, s] * values[s]
                out[k, e, low:rows] = total

    def drain(q):
        for h in range(2):
            for to in others(1 - h):
                z_copy(q, h, to, mine[1 - h]).wait_send()
            for c in range(rounds - YBUFS, rounds):
                for to in others(h):
                    y_copy(q, c, h, to, mine[h]).wait_send()

    for h in range(2):
        for to in others(h):
            meta(h, to, mine[h]).wait_send()
    drain(2)
    drain(0)
    pl.when(core == 1)(lambda: drain(1))
    back_each(lambda copy: copy.wait_send())

    @pl.loop(0, rounds)
    def _(c):
        late_each(c, lambda copy: copy.wait_send())

    @pl.loop(rounds - PBUFS, rounds)
    def _(c):
        for to in times():
            early_copy(c, to, tau).wait_send()


def plan(target, owners, ny, nz):
    count = target.shape[0]
    per = count // CHUNKS
    each = CAP // CHUNKS
    index = jnp.arange(count, dtype=jnp.int32)
    key = target * 256 + index
    rank = jnp.sum((key[None, :] < key[:, None]).astype(jnp.int32), axis=1)
    ordered = jnp.sum(jnp.where(rank[:, None] == index[None, :], key[:, None], 0), axis=0)
    ordered = ordered.reshape(per, CHUNKS).T
    part = ordered & 255
    tile = ordered >> 8
    same = (tile[:, 1:] == tile[:, :-1]).astype(jnp.int32)
    none = jnp.zeros((CHUNKS, 1), jnp.int32)
    keep = jnp.concatenate([none, same], axis=1)
    last = 1 - jnp.concatenate([same, none], axis=1)
    owner = tile // CHI_DEV
    value = jnp.where(last != 0, tile - owner * CHI_DEV, -1)
    d = jnp.arange(owners, dtype=jnp.int32)
    start = jnp.sum((owner[:, None, :] < d[None, :, None]).astype(jnp.int32), axis=2)
    place = start[:, :, None] + jnp.arange(each, dtype=jnp.int32)
    within = jnp.arange(per, dtype=jnp.int32)
    hit = (place[..., None] == within) & (owner[:, None, None, :] == d[None, :, None, None])
    goal = jnp.sum(jnp.where(hit, value[:, None, None, :] + 1, 0), axis=3) - 1
    place = jnp.minimum(place, per - 1)
    goal = goal.reshape(CHUNKS, nz, ny, each)
    zs = jnp.arange(nz, dtype=jnp.int32)[None, :, None, None] * CHI_DEV
    ys = jnp.arange(ny, dtype=jnp.int32)[None, None, :, None] * CHI_DEV
    to_y = jnp.where(goal >= 0, goal + zs, -1).transpose(2, 1, 3, 0).reshape(ny, nz * each, CHUNKS)
    to_z = jnp.where(goal >= 0, goal + ys, -1).transpose(1, 2, 3, 0).reshape(nz, ny * each, CHUNKS)
    both = jnp.stack([to_y, to_z])
    both = jnp.broadcast_to(both[..., None], both.shape + (128,))
    return part.reshape(-1), keep.reshape(-1), place.reshape(-1), both


def body(occupied, virtual, cos_weights, pair_occ, pair_virt, partial_target_tile):
    owners = lax.axis_size("tile")
    groups = lax.axis_size("tau")
    size = occupied.shape[2]
    terms = pair_occ.shape[1]
    count = partial_target_tile.shape[0]
    freqs = cos_weights.shape[0]
    ny = 1
    while 2 * ny * 2 * ny <= owners:
        ny *= 2
    nz = owners // ny
    rows = size // groups
    per = count // CHUNKS
    slots = ny * (CAP // CHUNKS)
    half = freqs // 2
    low = rows // 2
    nx = groups // 2
    part, keep, place, both = plan(partial_target_tile, owners, ny, nz)
    smem = pl.BlockSpec(memory_space=pltpu.SMEM)
    vmem = pl.BlockSpec(memory_space=pltpu.VMEM)
    dma = pltpu.SemaphoreType.DMA
    f32 = jnp.float32
    return pl.pallas_call(
        functools.partial(main_kernel, ny, nz, groups, terms),
        out_shape=jax.ShapeDtypeStruct((freqs, CHI_DEV, rows, size), f32),
        in_specs=[smem] * 6 + [vmem] * 3,
        out_specs=vmem,
        scratch_shapes=[
            pltpu.VMEM((PBUFS, groups, per, low, size), f32),
            pltpu.VMEM((CHUNKS, nx, per, low, size), f32),
            pltpu.VMEM((per, nx, low, size), f32),
            pltpu.VMEM((RING, groups, per, low, size), f32),
            pltpu.VMEM((CHUNKS, groups, per, low, size), f32),
            pltpu.VMEM((per, freqs, low, size), f32),
            pltpu.VMEM((3, YBUFS, 2, ny, slots, half, low, size), f32),
            pltpu.VMEM((3, RING, 2, ny, slots, half, low, size), f32),
            pltpu.VMEM((2, ny * (slots + 1), half, low, size), f32),
            pltpu.VMEM((3, 2, ny, CHI_DEV, half, low, size), f32),
            pltpu.VMEM((3, 2, ny, CHI_DEV, half, low, size), f32),
            pltpu.VMEM((nx, CHI_DEV, low, size), f32),
            pltpu.VMEM((groups, CHI_DEV, low, size), f32),
            pltpu.VMEM((2, ny, slots, CHUNKS, size), jnp.int32),
            pltpu.VMEM((2, CHUNKS, size), jnp.int32),
            pltpu.SMEM((2, CHUNKS, size), jnp.int32),
            dma((PBUFS * groups,)),
            dma((RING * groups,)),
            dma((CHUNKS * nx,)),
            dma((CHUNKS * groups,)),
            dma((3 * YBUFS * 8,)),
            dma((3 * RING * 8,)),
            dma((3 * 8,)),
            dma((3 * 8,)),
            dma((nx,)),
            dma((groups,)),
            dma((8,)),
            dma((8,)),
            dma,
        ],
        compiler_params=pltpu.CompilerParams(
            collective_id=0, has_side_effects=True, vmem_limit_bytes=62 * 1024 * 1024),
    )(cos_weights, pair_occ.reshape(-1), pair_virt.reshape(-1), part, keep, place,
      occupied[0], virtual[0], both)


def solution(mesh):
    in_specs = (
        P("tau", "tile", None, None),
        P("tau", "tile", None, None),
        P(),
        P("tile", None),
        P("tile", None),
        P("tile"),
    )
    out_specs = P(None, "tile", "tau", None)
    return jax.shard_map(body, mesh=mesh, in_specs=in_specs, out_specs=out_specs, check_vma=False)
```

time: 209 us -> 171 us (0.82)
  Pallas kernels: 198 us -> 160 us
    pallas_call x1, Pallas kernels: 198 us -> 160 us  [body(): pl.pallas_call(functools.partial(main_kernel, ny, nz, groups, terms), out...]
where the time goes in v2:
time: 171 us
  Pallas kernels  160 us (94%)
  local copies, waits for them, and re-layouts  8.83 us (5%)
  other arithmetic  2.18 us (1%)
    pallas_call x1, Pallas kernels, body(): pl.pallas_call(functools.partial(main_kernel, ny, nz, groups, terms), out...  160 us
    unnamed x3, local copies, waits for them, and re-layouts  3.92 us

profile of v2, /device:TPU:1, one launch (start us, length us, event | category | flops | bytes accessed | tf_op | source)
XLA Modules:
  0.0 170.7 jit_solution(7269242988319881027)
XLA Ops:
  0.0 0.7 iota_add_fusion.1
  0.7 0.2 convert_reduce_fusion
  0.9 0.1 select_reduce_fusion.1
  1.0 0.1 shift_right_arithmetic.14
  1.1 0.1 copy.41
  1.2 0.1 fusion.2
  1.3 0.1 select_add_fusion
  1.3 0.7 reshape.59.keep
  2.0 0.2 convert_reduce_fusion.1
  2.2 0.1 and.27
  2.4 0.7 reshape.58.part
  3.1 0.8 copy.38
  3.9 0.7 reshape.56.occ_idx
  4.6 0.8 copy.39
  5.4 0.7 reshape.57.virt_idx
  6.1 0.1 iota_add_fusion
  6.2 0.1 copy.42
  6.3 0.6 select_reduce_fusion
  6.9 0.8 min.12.place
  7.7 0.1 copy.44
  7.7 0.1 select_bitcast_fusion.1
  7.9 0.9 broadcast_in_dim.27.tv
  8.8 159.6 %shard_map.64 = f32[4,32,16,128]{3,2,1,0:T(8,128)} custom-call(f32[4,8]{1,0:T(4,128)} %weights.1, s32[3072]{0:T(1024)} %reshape.56.occ_idx, s32[3072]{0:T(1024)} %reshape.57.virt_idx, s32[192]{0:T(256)} %reshape.58.part, s32[192]{0:T(256)} %reshape.59.keep, s32[384]{0:T(512)} %min.12.place, bf16[128,128,128]{2,1,0:T(8,128)(2,1)} %bitcast.15, ...), custom_call_target="tpu_custom_call" | custom-call | tf_op jit(solution)/shard_map/pallas_call | solution.py:432
  168.4 2.3 %copy.50 = f32[4,32,16,128]{3,2,1,0:T(8,128)} copy(f32[4,32,16,128]{3,2,1,0:T(8,128)} %shard_map.64) | data formatting | bytes 2097152
  (9 shorter events, 0.1 us)

commit v3 on v2

v3 whole, which is shorter than its diff:
```python
import functools
import math

import jax
import jax.numpy as jnp
from jax import lax
from jax.experimental import pallas as pl
from jax.experimental.pallas import tpu as pltpu
from jax.sharding import PartitionSpec as P

CHI_DEV = 32
CAP = 24
CHUNKS = 8
PBUFS = 4
YBUFS = 2
RING = 4
GROUP = 4
MESH = pl.DeviceIdType.MESH


def main_kernel(ny, nz, groups, terms,
                weights, occ_idx, virt_idx, part, keep, place, occ, virt, tv,
                out,
                early, late, timed, x_early, x_late, freq, ybuf, yrecv, work, scan, dense, zrecv,
                final, back, trecv, order_v, spot_v, order, spot,
                e_send, e_recv, l_send, l_recv, y_send, y_recv, z_send, z_recv,
                b_send, b_recv, t_send, t_recv, tbl_sem):
    tau = lax.axis_index("tau")
    tile = lax.axis_index("tile")
    x, core = tau // 2, tau % 2
    nx = groups // 2
    z, y = tile // ny, tile % ny
    mine = (y, z)
    sizes = (ny, nz)
    freqs, _, rows, width = out.shape
    low = rows // 2
    half = freqs // 2
    per = freq.shape[0]
    slots = yrecv.shape[4]
    each = slots // ny
    rounds = CHUNKS
    span = work.shape[2]
    share = slots * GROUP

    def peer(h, i):
        return {"tile": z * ny + i if h == 0 else i * ny + y}

    def others(h):
        return [(mine[h] + step) % sizes[h] for step in range(1, sizes[h])]

    def times():
        return [(tau + step) % groups for step in range(1, groups)]

    barrier = pltpu.get_barrier_semaphore()
    for to in times():
        pl.semaphore_signal(barrier, inc=1, device_id={"tau": to}, device_id_type=MESH)
    for h in range(2):
        for to in others(h):
            pl.semaphore_signal(barrier, inc=1, device_id=peer(h, to), device_id_type=MESH)
    pl.semaphore_wait(barrier, groups - 1 + ny - 1 + nz - 1)

    def meta(h, to, at):
        return pltpu.make_async_remote_copy(
            src_ref=tv.at[h * 4 + to], dst_ref=trecv.at[h * 4 + mine[h]],
            send_sem=t_send.at[h * 4 + to], recv_sem=t_recv.at[h * 4 + at],
            device_id=peer(h, to), device_id_type=MESH)

    def early_copy(c, to, source):
        return pltpu.make_async_remote_copy(
            src_ref=early.at[c % PBUFS, to], dst_ref=x_early.at[c, source],
            send_sem=e_send.at[c % PBUFS * groups + to],
            recv_sem=e_recv.at[c * groups + source],
            device_id={"tau": to}, device_id_type=MESH)

    def late_copy(c, dest, source):
        return pltpu.make_async_remote_copy(
            src_ref=late.at[c, dest], dst_ref=x_late.at[c, source],
            send_sem=l_send.at[c * nx + dest],
            recv_sem=l_recv.at[c * groups + source],
            device_id={"tau": 2 * dest + 1}, device_id_type=MESH)

    def late_each(c, act):
        for step in range(nx):
            dest = (x + step) % nx
            if step == 0:
                @pl.when(core == 0)
                def _():
                    act(late_copy(c, dest, tau))
            else:
                act(late_copy(c, dest, tau))

    def y_copy(q, n, h, to, source):
        return pltpu.make_async_remote_copy(
            src_ref=ybuf.at[q, n % YBUFS, h, to], dst_ref=yrecv.at[q, n % RING, h, source],
            send_sem=y_send.at[((q * YBUFS + n % YBUFS) * 2 + h) * 4 + to],
            recv_sem=y_recv.at[((q * RING + n % RING) * 2 + h) * 4 + source],
            device_id=peer(h, to), device_id_type=MESH)

    def z_copy(q, h, to, source):
        return pltpu.make_async_remote_copy(
            src_ref=dense.at[q, h, to], dst_ref=zrecv.at[q, h, source],
            send_sem=z_send.at[(q * 2 + h) * 4 + to],
            recv_sem=z_recv.at[(q * 2 + h) * 4 + source],
            device_id=peer(1 - h, to), device_id_type=MESH)

    def back_copy(dest, source):
        return pltpu.make_async_remote_copy(
            src_ref=final.at[dest], dst_ref=back.at[source],
            send_sem=b_send.at[dest], recv_sem=b_recv.at[source],
            device_id={"tau": 2 * dest}, device_id_type=MESH)

    def back_each(act):
        for step in range(nx):
            dest = (x + step) % nx
            if step == 0:
                @pl.when(core == 1)
                def _():
                    act(back_copy(dest, tau))
            else:
                act(back_copy(dest, tau))

    for h in range(2):
        for to in others(h):
            meta(h, to, mine[h]).start()
        trecv[h * 4 + mine[h]] = tv[h * 4 + mine[h]]
    scan[span] = jnp.zeros((half, low, width), jnp.float32)

    def compute(c):
        slot = c % PBUFS

        def one(i, last):
            p = part[c, i]
            left = [occ[occ_idx[j, p]] for j in range(terms)]
            right = [virt[virt_idx[j, p]] for j in range(terms)]
            acc = jnp.dot(
                jnp.concatenate(left, axis=1),
                jnp.concatenate(right, axis=0),
                preferred_element_type=jnp.float32,
            )
            acc = acc + jnp.where(keep[c, i] != 0, last, 0.0)
            for g in range(groups):
                early[slot, g, i] = acc[g * rows:g * rows + low]
                upper = acc[g * rows + low:(g + 1) * rows]
                if g % 2 == 0:
                    timed[i, g // 2] = upper
                else:
                    late[c, g // 2, i] = upper
            return acc

        lax.fori_loop(0, per, one, jnp.zeros((rows * groups, width), jnp.float32),
                      unroll=math.gcd(per, 4))

    def transform(landed, at):
        @pl.loop(0, per, unroll=2)
        def _(i):
            values = [landed[at, s, i] for s in range(groups)]
            for k in range(freqs):
                total = weights[k, 0] * values[0]
                for s in range(1, groups):
                    total += weights[k, s] * values[s]
                freq[i, k] = total

    def send_y(q, n, c, values):
        @pl.when(n >= YBUFS)
        def _():
            for h in range(2):
                for to in others(h):
                    y_copy(q, n - YBUFS, h, to, mine[h]).wait_send()

        @pl.loop(0, nz)
        def _(dz):
            for dy in range(ny):
                for m in range(each):
                    i = place[c, (dz * ny + dy) * each + m]
                    ybuf[q, n % YBUFS, 0, dy, dz * each + m] = values[i, 0:half]
                    ybuf[q, n % YBUFS, 1, dz, dy * each + m] = values[i, half:freqs]

        for h in range(2):
            for to in others(h):
                y_copy(q, n, h, to, mine[h]).start()
            for e in range(slots):
                yrecv[q, n % RING, h, mine[h], e] = ybuf[q, n % YBUFS, h, mine[h], e]

    def tables():
        for h in range(2):
            for s in others(h):
                meta(h, s, s).wait_recv()
            for g in range(CHUNKS // GROUP):
                lane = lax.broadcasted_iota(jnp.int32, (share, width), 1)
                local = lax.broadcasted_iota(jnp.int32, (share, width), 0)
                goal = jnp.concatenate([
                    jnp.sum(jnp.where(lane == local + g * share, trecv[h * 4 + s][0:1], 0),
                            axis=1, keepdims=True) for s in range(sizes[h])], axis=0)
                index = lax.broadcasted_iota(jnp.int32, (span, 1), 0)
                valid = goal >= 0
                goal = jnp.where(valid, goal, 200)
                column = goal * 256 + index
                wide = (span, 2 * width)
                across = lax.broadcasted_iota(jnp.int32, wide, 1)
                down = lax.broadcasted_iota(jnp.int32, wide, 0)
                column_w = jnp.broadcast_to(column, wide)
                goal_w = jnp.broadcast_to(goal, wide)
                row = jnp.sum(jnp.where(across == down, column_w, 0), axis=0, keepdims=True)
                row_goal = jnp.sum(jnp.where(across == down, goal_w, 0), axis=0, keepdims=True)
                before = (row < column_w) & (across < span)
                rank = jnp.sum(jnp.where(before, 1, 0), axis=1, keepdims=True)
                joined = jnp.max(jnp.where(before & (row_goal == goal_w), 1, 0),
                                 axis=1, keepdims=True)
                entry = index + 1024 * joined
                entry = jnp.sum(jnp.where(rank == across, entry, 0), axis=0, keepdims=True)
                at = h * (CHUNKS // GROUP) + g
                order_v[at:at + 1] = entry
                found = jnp.where((goal == across[:, :width]) & valid, rank, -1)
                found = jnp.max(found, axis=0, keepdims=True)
                found = jnp.where(found < 0, span, found)
                spot_v[at:at + 1] = found
        for i, (source, into) in enumerate(((order_v, order), (spot_v, spot))):
            copy = pltpu.make_async_copy(source, into, tbl_sem.at[i])
            copy.start()
            copy.wait()

    def collect(q, n):
        for h in range(2):
            for s in others(h):
                y_copy(q, n, h, s, s).wait_recv()
            for s in range(sizes[h]):
                for e in range(slots):
                    work[q, h, s * share + e * GROUP + n % GROUP] = yrecv[q, n % RING, h, s, e]

    def densify(q, stream, g):
        for h in range(2):
            at = h * (CHUNKS // GROUP) + g

            def one(r, last):
                entry = order[at, r]
                value = work[q, h, entry & 1023]
                value = value + jnp.where(entry >= 1024, last, 0.0)
                scan[r] = value
                return value

            lax.fori_loop(0, span, one, jnp.zeros((half, low, width), jnp.float32), unroll=8)

            @pl.loop(0, sizes[1 - h])
            def _(o):
                @pl.loop(0, CHI_DEV, unroll=8)
                def _(e):
                    value = scan[spot[at, o * CHI_DEV + e]]
                    if g:
                        value = value + dense[stream, h, o, e]
                    dense[stream, h, o, e] = value

    def send_z(q):
        for h in range(2):
            for to in others(1 - h):
                z_copy(q, h, to, mine[1 - h]).start()

    def finish(q, store):
        for h in range(2):
            for s in others(1 - h):
                z_copy(q, h, s, s).wait_recv()
            own = mine[1 - h]

            @pl.loop(0, CHI_DEV, unroll=4)
            def _(e):
                total = dense[q, h, own, e]
                for s in others(1 - h):
                    total += zrecv[q, h, s, e]
                for k in range(half):
                    store(h * half + k, e, total[k])

    def store_early(k, e, value):
        out[k, e, 0:low] = value

    def store_late(k, e, value):
        out[k, e, low:rows] = value

    def store_final(k, e, value):
        final[k, e] = value

    def when(condition):
        return pl.when(condition)

    @pl.loop(0, 2 * rounds + 3)
    def _(t):
        @when(t < rounds)
        def _():
            @when(t >= PBUFS)
            def _():
                for to in times():
                    early_copy(t - PBUFS, to, tau).wait_send()
            compute(t)
            for to in times():
                early_copy(t, to, tau).start()

        @when(t == rounds - 1)
        def _():
            @pl.loop(0, rounds)
            def _(c):
                late_each(c, lambda copy: copy.start())

        @when(t < rounds)
        def _():
            send_y(1, t, t, timed)

            @pl.loop(0, per, unroll=4)
            def _(i):
                x_early[t, tau, i] = early[t % PBUFS, tau, i]

        @when((t >= 2) & (t < rounds + 2))
        def _():
            c = t - 2
            for s in times():
                early_copy(c, s, s).wait_recv()
            transform(x_early, c)
            send_y(0, c, c, freq)

        @when((t >= rounds + 2) & (t < 2 * rounds + 2) & (core == 1))
        def _():
            c = t - rounds - 2

            @pl.loop(0, per, unroll=4)
            def _(i):
                x_late[c, tau, i] = late[c, x, i]
            for s in times():
                late_copy(c, x, s).wait_recv()
            transform(x_late, c)
            send_y(1, c + rounds, c, freq)

        @when(t == 1)
        def _():
            tables()

        @when((t >= 1) & (t < rounds + 1))
        def _():
            collect(1, t - 1)

        @when(t == GROUP)
        def _():
            densify(1, 2, 0)

        @when(t == rounds)
        def _():
            densify(1, 2, 1)
            send_z(2)

        @when((t >= 3) & (t < rounds + 3))
        def _():
            collect(0, t - 3)

        @when(t == GROUP + 2)
        def _():
            densify(0, 0, 0)

        @when(t == rounds + 2)
        def _():
            densify(0, 0, 1)
            send_z(0)

        @when(t == rounds + 3)
        def _():
            finish(2, store_final)
            back_each(lambda copy: copy.start())

        @when((t >= rounds + 3) & (core == 1))
        def _():
            collect(1, t - 3)

        @when((t == rounds + 2 + GROUP) & (core == 1))
        def _():
            densify(1, 1, 0)

        @when(t == rounds + 3 + GROUP)
        def _():
            finish(0, store_early)

    @when(core == 1)
    def _():
        densify(1, 1, 1)
        send_z(1)
        finish(1, store_late)

    @when(core == 0)
    def _():
        @pl.loop(0, CHI_DEV, unroll=4)
        def _(e):
            back[tau, e] = final[x, e]
        for s in times():
            back_copy(x, s).wait_recv()

        @pl.loop(0, CHI_DEV, unroll=2)
        def _(e):
            values = [back[s, e] for s in range(groups)]
            for k in range(freqs):
                total = weights[k, 0] * values[0]
                for s in range(1, groups):
                    total += weights[k, s] * values[s]
                out[k, e, low:rows] = total

    def drain_z(q):
        for h in range(2):
            for to in others(1 - h):
                z_copy(q, h, to, mine[1 - h]).wait_send()

    def drain_y(q):
        for h in range(2):
            for n in range(YBUFS):
                for to in others(h):
                    y_copy(q, n, h, to, mine[h]).wait_send()

    for h in range(2):
        for to in others(h):
            meta(h, to, mine[h]).wait_send()
    drain_z(2)
    drain_z(0)
    drain_y(0)
    drain_y(1)
    pl.when(core == 1)(lambda: drain_z(1))
    back_each(lambda copy: copy.wait_send())

    @pl.loop(0, rounds)
    def _(c):
        late_each(c, lambda copy: copy.wait_send())

    @pl.loop(rounds - PBUFS, rounds)
    def _(c):
        for to in times():
            early_copy(c, to, tau).wait_send()


def plan(target, owners, ny, nz):
    count = target.shape[0]
    per = count // CHUNKS
    each = CAP // CHUNKS
    index = jnp.arange(count, dtype=jnp.int32)
    key = target * 256 + index
    rank = jnp.sum((key[None, :] < key[:, None]).astype(jnp.int32), axis=1)
    at = jnp.arange(per)[None, :] * CHUNKS + jnp.arange(CHUNKS)[:, None]
    ordered = jnp.sum(jnp.where(rank == at[..., None], key, 0), axis=2)
    part = ordered & 255
    tile = ordered >> 8
    same = (tile[:, 1:] == tile[:, :-1]).astype(jnp.int32)
    none = jnp.zeros((CHUNKS, 1), jnp.int32)
    keep = jnp.concatenate([none, same], axis=1)
    last = 1 - jnp.concatenate([same, none], axis=1)
    owner = tile // CHI_DEV
    value = jnp.where(last != 0, tile - owner * CHI_DEV, -1)
    j = jnp.arange(owners * each, dtype=jnp.int32)
    d, m = j // each, j % each
    place = jnp.sum((owner[:, None, :] < d[None, :, None]).astype(jnp.int32), axis=2) + m
    within = jnp.arange(per, dtype=jnp.int32)
    hit = (place[..., None] == within) & (owner[:, None, :] == d[None, :, None])
    goal = jnp.sum(jnp.where(hit, value[:, None, :] + 1, 0), axis=2) - 1
    place = jnp.minimum(place, per - 1)
    goal = goal.reshape(CHUNKS // GROUP, GROUP, nz, ny, each)
    zs = jnp.arange(nz, dtype=jnp.int32)[:, None, None] * CHI_DEV
    ys = jnp.arange(ny, dtype=jnp.int32)[None, :, None] * CHI_DEV
    to_y = jnp.where(goal >= 0, goal + zs, -1).transpose(3, 0, 2, 4, 1).reshape(ny, -1)
    to_z = jnp.where(goal >= 0, goal + ys, -1).transpose(2, 0, 3, 4, 1).reshape(nz, -1)
    both = jnp.concatenate([to_y, to_z])
    both = jnp.pad(both, ((0, 0), (0, 128 - both.shape[1])))
    both = jnp.broadcast_to(both[:, None], (both.shape[0], 8, 128))
    return part, keep, place, both


def body(occupied, virtual, cos_weights, pair_occ, pair_virt, partial_target_tile):
    owners = lax.axis_size("tile")
    groups = lax.axis_size("tau")
    size = occupied.shape[2]
    terms = pair_occ.shape[1]
    count = partial_target_tile.shape[0]
    freqs = cos_weights.shape[0]
    ny = 1
    while 2 * ny * 2 * ny <= owners:
        ny *= 2
    nz = owners // ny
    rows = size // groups
    per = count // CHUNKS
    slots = ny * (CAP // CHUNKS)
    half = freqs // 2
    low = rows // 2
    nx = groups // 2
    span = ny * slots * GROUP
    part, keep, place, both = plan(partial_target_tile, owners, ny, nz)
    smem = pl.BlockSpec(memory_space=pltpu.SMEM)
    vmem = pl.BlockSpec(memory_space=pltpu.VMEM)
    dma = pltpu.SemaphoreType.DMA
    f32 = jnp.float32
    return pl.pallas_call(
        functools.partial(main_kernel, ny, nz, groups, terms),
        out_shape=jax.ShapeDtypeStruct((freqs, CHI_DEV, rows, size), f32),
        in_specs=[smem] * 6 + [vmem] * 3,
        out_specs=vmem,
        scratch_shapes=[
            pltpu.VMEM((PBUFS, groups, per, low, size), f32),
            pltpu.VMEM((CHUNKS, nx, per, low, size), f32),
            pltpu.VMEM((per, nx, low, size), f32),
            pltpu.VMEM((CHUNKS, groups, per, low, size), f32),
            pltpu.VMEM((CHUNKS, groups, per, low, size), f32),
            pltpu.VMEM((per, freqs, low, size), f32),
            pltpu.VMEM((2, YBUFS, 2, ny, slots, half, low, size), f32),
            pltpu.VMEM((2, RING, 2, ny, slots, half, low, size), f32),
            pltpu.VMEM((2, 2, span, half, low, size), f32),
            pltpu.VMEM((span + 1, half, low, size), f32),
            pltpu.VMEM((3, 2, ny, CHI_DEV, half, low, size), f32),
            pltpu.VMEM((3, 2, ny, CHI_DEV, half, low, size), f32),
            pltpu.VMEM((nx, CHI_DEV, low, size), f32),
            pltpu.VMEM((groups, CHI_DEV, low, size), f32),
            pltpu.VMEM((8, 8, size), jnp.int32),
            pltpu.VMEM((8, 2 * size), jnp.int32),
            pltpu.VMEM((8, size), jnp.int32),
            pltpu.SMEM((8, 2 * size), jnp.int32),
            pltpu.SMEM((8, size), jnp.int32),
            dma((PBUFS * groups,)),
            dma((CHUNKS * groups,)),
            dma((CHUNKS * nx,)),
            dma((CHUNKS * groups,)),
            dma((2 * YBUFS * 8,)),
            dma((2 * RING * 8,)),
            dma((3 * 8,)),
            dma((3 * 8,)),
            dma((nx,)),
            dma((groups,)),
            dma((8,)),
            dma((8,)),
            dma((2,)),
        ],
        compiler_params=pltpu.CompilerParams(
            collective_id=0, has_side_effects=True, vmem_limit_bytes=62 * 1024 * 1024),
    )(cos_weights, pair_occ.T, pair_virt.T, part, keep, place,
      occupied[0], virtual[0], both)


def solution(mesh):
    in_specs = (
        P("tau", "tile", None, None),
        P("tau", "tile", None, None),
        P(),
        P("tile", None),
        P("tile", None),
        P("tile"),
    )
    out_specs = P(None, "tile", "tau", None)
    return jax.shard_map(body, mesh=mesh, in_specs=in_specs, out_specs=out_specs, check_vma=False)
```

time: 171 us -> 161 us (0.942)
  Pallas kernels: 160 us -> 154 us
  local copies, waits for them, and re-layouts: 8.83 us -> 3.87 us
    pallas_call x1, Pallas kernels: 160 us -> 154 us  [body(): pl.pallas_call(functools.partial(main_kernel, ny, nz, groups, terms), out...]
    reshape x4 -> x2, local copies, waits for them, and re-layouts: 2.72 us -> 0.22 us  [the longest x1 0.11 us: plan(): jnp.where(goal >= 0, goal + ys, -1).transpose(2, 0, 3, 4, 1).reshape(nz, -1)]
    unnamed x3 -> x1, local copies, waits for them, and re-layouts: 3.92 us -> 2.29 us
where the time goes in v3:
time: 161 us
  Pallas kernels  154 us (96%)
  local copies, waits for them, and re-layouts  3.87 us (2%)
  other arithmetic  2.86 us (2%)
    pallas_call x1, Pallas kernels, body(): pl.pallas_call(functools.partial(main_kernel, ny, nz, groups, terms), out...  154 us

profile of v3, /device:TPU:1, one launch (start us, length us, event | category | flops | bytes accessed | tf_op | source)
XLA Modules:
  0.0 161.0 jit_solution(4895649525024012483)
XLA Ops:
  0.0 0.7 iota_add_fusion.1
  0.7 0.2 convert_reduce_fusion
  0.9 0.3 select_reduce_fusion
  1.2 0.1 fusion.2
  1.3 0.7 select_add_fusion
  2.0 0.1 convert_reduce_fusion.1
  2.1 0.6 broadcast_minimum_fusion
  2.7 0.1 select_reduce_fusion.1
  2.8 0.1 sub.32
  2.9 0.1 select_bitcast_fusion.1
  3.0 0.3 copy.10
  3.4 0.1 reshape.107
  3.5 0.3 copy.11
  3.8 0.1 reshape.108
  3.9 0.6 broadcast_in_dim.30.tv
  4.5 154.2 %shard_map.64 = f32[4,32,16,128]{3,2,1,0:T(8,128)} custom-call(f32[4,8]{1,0:T(4,128)} %weights.1, s32[16,192]{1,0:T(8,128)} %bitcast.10, s32[16,192]{1,0:T(8,128)} %bitcast.11, s32[8,24]{1,0:T(8,128)} %get-tuple-element.11.part, s32[8,24]{1,0:T(8,128)} %get-tuple-element.12.keep, s32[8,48]{1,0:T(8,128)} %get-tuple-element.5.place, ...), custom_call_target="tpu_custom_call" | custom-call | tf_op jit(solution)/shard_map/pallas_call | solution.py:488
  158.7 2.3 %copy.13 = f32[4,32,16,128]{3,2,1,0:T(8,128)} copy(f32[4,32,16,128]{3,2,1,0:T(8,128)} %shard_map.64) | data formatting | bytes 2097152
  (9 shorter events, 0.1 us)

commit v4 on v3

--- a/solution.py
+++ b/solution.py
@@ -12,19 +12,24 @@
 CAP = 24
 CHUNKS = 8
 PBUFS = 4
-YBUFS = 2
-RING = 4
+YBUFS = (2, 4)
+RINGS = (4, 8)
+XRING = 6
+PARTS = 2
 GROUP = 4
+LATER = 3
+FSTEP = 5
+LOADS = 4
 MESH = pl.DeviceIdType.MESH
 
 
 def main_kernel(ny, nz, groups, terms,
-                weights, occ_idx, virt_idx, part, keep, place, occ, virt, tv,
+                weights_in, occ_idx_in, virt_idx_in, steps_in, tv_in, occ_hbm, virt_hbm,
                 out,
-                early, late, timed, x_early, x_late, freq, ybuf, yrecv, work, scan, dense, zrecv,
+                occ, virt, weights, occ_idx, virt_idx, steps, tv, early, late, timed, x_early, x_late, freq, y_out_first, y_out_second, y_first, y_second, work, scan, dense, zrecv,
                 final, back, trecv, order_v, spot_v, order, spot,
                 e_send, e_recv, l_send, l_recv, y_send, y_recv, z_send, z_recv,
-                b_send, b_recv, t_send, t_recv, tbl_sem):
+                b_send, b_recv, t_send, t_recv, tbl_sem, load_sem):
     tau = lax.axis_index("tau")
     tile = lax.axis_index("tile")
     x, core = tau // 2, tau % 2
@@ -36,7 +41,7 @@
     low = rows // 2
     half = freqs // 2
     per = freq.shape[0]
-    slots = yrecv.shape[4]
+    slots = y_first.shape[3]
     each = slots // ny
     rounds = CHUNKS
     span = work.shape[2]
@@ -50,6 +55,30 @@
 
     def times():
         return [(tau + step) % groups for step in range(1, groups)]
+
+    landing = (y_first, y_second)
+    ring = (y_first.shape[0], y_second.shape[0])
+    base = (0, ring[0])
+    leaving = (y_out_first, y_out_second)
+    outs = (y_out_first.shape[0], y_out_second.shape[0])
+    out_base = (0, outs[0])
+    part_size = occ.shape[0] // LOADS
+
+    def load(i):
+        at = pl.ds(i % LOADS * part_size, part_size)
+        source, into = ((occ_hbm, occ), (virt_hbm, virt))[i // LOADS]
+        return pltpu.make_async_copy(source.at[at], into.at[at], load_sem.at[i])
+
+    small = [
+        pltpu.make_async_copy(source, into, load_sem.at[2 * LOADS + i])
+        for i, (source, into) in enumerate((
+            (tv_in, tv), (occ_idx_in, occ_idx), (virt_idx_in, virt_idx),
+            (steps_in, steps), (weights_in, weights)))
+    ]
+    for copy in small:
+        copy.start()
+    for i in range(2 * LOADS):
+        load(i).start()
 
     barrier = pltpu.get_barrier_semaphore()
     for to in times():
@@ -65,11 +94,12 @@
             send_sem=t_send.at[h * 4 + to], recv_sem=t_recv.at[h * 4 + at],
             device_id=peer(h, to), device_id_type=MESH)
 
-    def early_copy(c, to, source):
+    def early_copy(c, to, source, at=None):
+        at = pl.ds(0, per) if at is None else at
         return pltpu.make_async_remote_copy(
-            src_ref=early.at[c % PBUFS, to], dst_ref=x_early.at[c, source],
+            src_ref=early.at[c % PBUFS, to, at], dst_ref=x_early.at[c % XRING, source, at],
             send_sem=e_send.at[c % PBUFS * groups + to],
-            recv_sem=e_recv.at[c * groups + source],
+            recv_sem=e_recv.at[c % XRING * groups + source],
             device_id={"tau": to}, device_id_type=MESH)
 
     def late_copy(c, dest, source):
@@ -91,9 +121,9 @@
 
     def y_copy(q, n, h, to, source):
         return pltpu.make_async_remote_copy(
-            src_ref=ybuf.at[q, n % YBUFS, h, to], dst_ref=yrecv.at[q, n % RING, h, source],
-            send_sem=y_send.at[((q * YBUFS + n % YBUFS) * 2 + h) * 4 + to],
-            recv_sem=y_recv.at[((q * RING + n % RING) * 2 + h) * 4 + source],
+            src_ref=leaving[q].at[n % outs[q], h, to], dst_ref=landing[q].at[n % ring[q], h, source],
+            send_sem=y_send.at[((out_base[q] + n % outs[q]) * 2 + h) * 4 + to],
+            recv_sem=y_recv.at[((base[q] + n % ring[q]) * 2 + h) * 4 + source],
             device_id=peer(h, to), device_id_type=MESH)
 
     def z_copy(q, h, to, source):
@@ -119,17 +149,21 @@
             else:
                 act(back_copy(dest, tau))
 
+    for copy in small:
+        copy.wait()
     for h in range(2):
         for to in others(h):
             meta(h, to, mine[h]).start()
         trecv[h * 4 + mine[h]] = tv[h * 4 + mine[h]]
     scan[span] = jnp.zeros((half, low, width), jnp.float32)
+    for i in range(2 * LOADS):
+        load(i).wait()
 
     def compute(c):
         slot = c % PBUFS
 
         def one(i, last):
-            p = part[c, i]
+            p = steps[c, i]
             left = [occ[occ_idx[j, p]] for j in range(terms)]
             right = [virt[virt_idx[j, p]] for j in range(terms)]
             acc = jnp.dot(
@@ -137,7 +171,7 @@
                 jnp.concatenate(right, axis=0),
                 preferred_element_type=jnp.float32,
             )
-            acc = acc + jnp.where(keep[c, i] != 0, last, 0.0)
+            acc = acc + jnp.where(steps[c, per + i] != 0, last, 0.0)
             for g in range(groups):
                 early[slot, g, i] = acc[g * rows:g * rows + low]
                 upper = acc[g * rows + low:(g + 1) * rows]
@@ -147,8 +181,17 @@
                     late[c, g // 2, i] = upper
             return acc
 
-        lax.fori_loop(0, per, one, jnp.zeros((rows * groups, width), jnp.float32),
-                      unroll=math.gcd(per, 4))
+        size = per // PARTS
+
+        def portion(k, last):
+            last = lax.fori_loop(
+                0, size, lambda i, last: one(k * size + i, last), last,
+                unroll=math.gcd(size, 4))
+            for to in times():
+                early_copy(c, to, tau, pl.ds(k * size, size)).start()
+            return last
+
+        lax.fori_loop(0, PARTS, portion, jnp.zeros((rows * groups, width), jnp.float32))
 
     def transform(landed, at):
         @pl.loop(0, per, unroll=2)
@@ -161,25 +204,25 @@
                 freq[i, k] = total
 
     def send_y(q, n, c, values):
-        @pl.when(n >= YBUFS)
+        @pl.when(n >= outs[q])
         def _():
             for h in range(2):
                 for to in others(h):
-                    y_copy(q, n - YBUFS, h, to, mine[h]).wait_send()
+                    y_copy(q, n - outs[q], h, to, mine[h]).wait_send()
 
         @pl.loop(0, nz)
         def _(dz):
             for dy in range(ny):
                 for m in range(each):
-                    i = place[c, (dz * ny + dy) * each + m]
-                    ybuf[q, n % YBUFS, 0, dy, dz * each + m] = values[i, 0:half]
-                    ybuf[q, n % YBUFS, 1, dz, dy * each + m] = values[i, half:freqs]
+                    i = steps[c, 2 * per + (dz * ny + dy) * each + m]
+                    leaving[q][n % outs[q], 0, dy, dz * each + m] = values[i, 0:half]
+                    leaving[q][n % outs[q], 1, dz, dy * each + m] = values[i, half:freqs]
 
         for h in range(2):
             for to in others(h):
                 y_copy(q, n, h, to, mine[h]).start()
             for e in range(slots):
-                yrecv[q, n % RING, h, mine[h], e] = ybuf[q, n % YBUFS, h, mine[h], e]
+                landing[q][n % ring[q], h, mine[h], e] = leaving[q][n % outs[q], h, mine[h], e]
 
     def tables():
         for h in range(2):
@@ -225,7 +268,7 @@
                 y_copy(q, n, h, s, s).wait_recv()
             for s in range(sizes[h]):
                 for e in range(slots):
-                    work[q, h, s * share + e * GROUP + n % GROUP] = yrecv[q, n % RING, h, s, e]
+                    work[q, h, s * share + e * GROUP + n % GROUP] = landing[q][n % ring[q], h, s, e]
 
     def densify(q, stream, g):
         for h in range(2):
@@ -280,7 +323,7 @@
     def when(condition):
         return pl.when(condition)
 
-    @pl.loop(0, 2 * rounds + 3)
+    @pl.loop(0, 2 * rounds + 2 + LATER)
     def _(t):
         @when(t < rounds)
         def _():
@@ -289,8 +332,6 @@
                 for to in times():
                     early_copy(t - PBUFS, to, tau).wait_send()
             compute(t)
-            for to in times():
-                early_copy(t, to, tau).start()
 
         @when(t == rounds - 1)
         def _():
@@ -304,14 +345,14 @@
 
             @pl.loop(0, per, unroll=4)
             def _(i):
-                x_early[t, tau, i] = early[t % PBUFS, tau, i]
+                x_early[t % XRING, tau, i] = early[t % PBUFS, tau, i]
 
         @when((t >= 2) & (t < rounds + 2))
         def _():
             c = t - 2
             for s in times():
                 early_copy(c, s, s).wait_recv()
-            transform(x_early, c)
+            transform(x_early, c % XRING)
             send_y(0, c, c, freq)
 
         @when((t >= rounds + 2) & (t < 2 * rounds + 2) & (core == 1))
@@ -341,42 +382,48 @@
         @when(t == rounds)
         def _():
             densify(1, 2, 1)
+
+        @when((t >= 3) & (t < rounds + 1))
+        def _():
+            collect(0, t - 3)
+
+        @when(t == GROUP + 2)
+        def _():
+            densify(0, 0, 0)
+
+        @when(t == rounds + 1)
+        def _():
             send_z(2)
 
-        @when((t >= 3) & (t < rounds + 3))
-        def _():
-            collect(0, t - 3)
-
-        @when(t == GROUP + 2)
-        def _():
-            densify(0, 0, 0)
-
-        @when(t == rounds + 2)
-        def _():
+        @when(t == rounds + 3)
+        def _():
+            collect(0, rounds - 2)
+            collect(0, rounds - 1)
             densify(0, 0, 1)
             send_z(0)
 
-        @when(t == rounds + 3)
+        @when(t == rounds + FSTEP)
         def _():
             finish(2, store_final)
             back_each(lambda copy: copy.start())
 
-        @when((t >= rounds + 3) & (core == 1))
-        def _():
-            collect(1, t - 3)
-
-        @when((t == rounds + 2 + GROUP) & (core == 1))
+        @when((t >= rounds + 2 + LATER) & (core == 1))
+        def _():
+            collect(1, t - 2 - LATER)
+
+        @when((t == rounds + 1 + LATER + GROUP) & (core == 1))
         def _():
             densify(1, 1, 0)
-
-        @when(t == rounds + 3 + GROUP)
-        def _():
-            finish(0, store_early)
 
     @when(core == 1)
     def _():
         densify(1, 1, 1)
         send_z(1)
+
+    finish(0, store_early)
+
+    @when(core == 1)
+    def _():
         finish(1, store_late)
 
     @when(core == 0)
@@ -403,7 +450,7 @@
 
     def drain_y(q):
         for h in range(2):
-            for n in range(YBUFS):
+            for n in range(outs[q]):
                 for to in others(h):
                     y_copy(q, n, h, to, mine[h]).wait_send()
 
@@ -459,7 +506,7 @@
     both = jnp.concatenate([to_y, to_z])
     both = jnp.pad(both, ((0, 0), (0, 128 - both.shape[1])))
     both = jnp.broadcast_to(both[:, None], (both.shape[0], 8, 128))
-    return part, keep, place, both
+    return jnp.concatenate([part, keep, place], axis=1), both
 
 
 def body(occupied, virtual, cos_weights, pair_occ, pair_virt, partial_target_tile):
@@ -480,25 +527,33 @@
     low = rows // 2
     nx = groups // 2
     span = ny * slots * GROUP
-    part, keep, place, both = plan(partial_target_tile, owners, ny, nz)
-    smem = pl.BlockSpec(memory_space=pltpu.SMEM)
+    steps, both = plan(partial_target_tile, owners, ny, nz)
     vmem = pl.BlockSpec(memory_space=pltpu.VMEM)
     dma = pltpu.SemaphoreType.DMA
     f32 = jnp.float32
     return pl.pallas_call(
         functools.partial(main_kernel, ny, nz, groups, terms),
         out_shape=jax.ShapeDtypeStruct((freqs, CHI_DEV, rows, size), f32),
-        in_specs=[smem] * 6 + [vmem] * 3,
+        in_specs=[pl.BlockSpec(memory_space=pl.ANY)] * 7,
         out_specs=vmem,
         scratch_shapes=[
+            pltpu.VMEM(occupied.shape[1:], occupied.dtype),
+            pltpu.VMEM(virtual.shape[1:], virtual.dtype),
+            pltpu.SMEM(cos_weights.shape, f32),
+            pltpu.SMEM((terms, count), jnp.int32),
+            pltpu.SMEM((terms, count), jnp.int32),
+            pltpu.SMEM(steps.shape, jnp.int32),
+            pltpu.VMEM(both.shape, jnp.int32),
             pltpu.VMEM((PBUFS, groups, per, low, size), f32),
             pltpu.VMEM((CHUNKS, nx, per, low, size), f32),
             pltpu.VMEM((per, nx, low, size), f32),
-            pltpu.VMEM((CHUNKS, groups, per, low, size), f32),
+            pltpu.VMEM((XRING, groups, per, low, size), f32),
             pltpu.VMEM((CHUNKS, groups, per, low, size), f32),
             pltpu.VMEM((per, freqs, low, size), f32),
-            pltpu.VMEM((2, YBUFS, 2, ny, slots, half, low, size), f32),
-            pltpu.VMEM((2, RING, 2, ny, slots, half, low, size), f32),
+            pltpu.VMEM((YBUFS[0], 2, ny, slots, half, low, size), f32),
+            pltpu.VMEM((YBUFS[1], 2, ny, slots, half, low, size), f32),
+            pltpu.VMEM((RINGS[0], 2, ny, slots, half, low, size), f32),
+            pltpu.VMEM((RINGS[1], 2, ny, slots, half, low, size), f32),
             pltpu.VMEM((2, 2, span, half, low, size), f32),
             pltpu.VMEM((span + 1, half, low, size), f32),
             pltpu.VMEM((3, 2, ny, CHI_DEV, half, low, size), f32),
@@ -511,11 +566,11 @@
             pltpu.SMEM((8, 2 * size), jnp.int32),
             pltpu.SMEM((8, size), jnp.int32),
             dma((PBUFS * groups,)),
-            dma((CHUNKS * groups,)),
+            dma((XRING * groups,)),
             dma((CHUNKS * nx,)),
             dma((CHUNKS * groups,)),
-            dma((2 * YBUFS * 8,)),
-            dma((2 * RING * 8,)),
+            dma((sum(YBUFS) * 8,)),
+            dma((sum(RINGS) * 8,)),
             dma((3 * 8,)),
             dma((3 * 8,)),
             dma((nx,)),
@@ -523,11 +578,12 @@
             dma((8,)),
             dma((8,)),
             dma((2,)),
+            dma((2 * LOADS + 5,)),
         ],
         compiler_params=pltpu.CompilerParams(
-            collective_id=0, has_side_effects=True, vmem_limit_bytes=62 * 1024 * 1024),
-    )(cos_weights, pair_occ.T, pair_virt.T, part, keep, place,
-      occupied[0], virtual[0], both)
+            collective_id=0, has_side_effects=True, vmem_limit_bytes=63 * 1024 * 1024),
+    )(cos_weights, pair_occ.T, pair_virt.T, steps,
+      both, occupied[0], virtual[0])
 
 
 def solution(mesh):

time: 161 us -> 151 us (0.938)
  Pallas kernels: 154 us -> 145 us
    pallas_call x1, Pallas kernels: 154 us -> 145 us  [body(): pl.pallas_call(functools.partial(main_kernel, ny, nz, groups, terms), out...]
where the time goes in v4:
time: 151 us
  Pallas kernels  145 us (96%)
  local copies, waits for them, and re-layouts  3.95 us (3%)
  other arithmetic  2.29 us (2%)
    pallas_call x1, Pallas kernels, body(): pl.pallas_call(functools.partial(main_kernel, ny, nz, groups, terms), out...  145 us

profile of v4, /device:TPU:1, one launch (start us, length us, event | category | flops | bytes accessed | tf_op | source)
XLA Modules:
  0.0 151.1 jit_solution(382980197498553386)
XLA Ops:
  0.0 0.1 pad.9.clone
  0.1 0.7 iota_add_fusion.1
  0.8 0.2 convert_reduce_fusion
  1.0 0.3 select_reduce_fusion
  1.3 0.1 fusion.2
  1.4 0.1 convert_reduce_fusion.1
  1.5 0.1 select_reduce_fusion.1
  1.6 0.7 pad_add_fusion.steps_in
  2.3 0.1 sub.32
  2.4 0.1 select_bitcast_fusion.1
  2.5 0.3 copy.10
  2.8 0.1 reshape.107
  3.0 0.3 copy.11
  3.3 0.1 reshape.108
  3.4 0.6 broadcast_in_dim.30.tv_in
  4.0 144.7 %shard_map.64 = f32[4,32,16,128]{3,2,1,0:T(8,128)} custom-call(f32[4,8]{1,0:T(4,128)} %weights_in.1, s32[16,192]{1,0:T(8,128)} %bitcast.11, s32[16,192]{1,0:T(8,128)} %bitcast.12, s32[8,96]{1,0:T(8,128)} %pad_add_fusion.steps_in, s32[8,8,128]{2,1,0:T(8,128)} %broadcast_in_dim.30.tv_in, bf16[128,128,128]{2,1,0:T(8,128)(2,1)} %bitcast.9, ...), custom_call_target="tpu_custom_call" | custom-call | tf_op jit(solution)/shard_map/pallas_call | solution.py:534
  148.8 2.3 %copy.13 = f32[4,32,16,128]{3,2,1,0:T(8,128)} copy(f32[4,32,16,128]{3,2,1,0:T(8,128)} %shard_map.64) | data formatting | bytes 2097152
  (11 shorter events, 0.1 us)

commit v5 on v4

--- a/solution.py
+++ b/solution.py
@@ -13,12 +13,13 @@
 CHUNKS = 8
 PBUFS = 4
 YBUFS = (2, 4)
-RINGS = (4, 8)
+RINGS = (6, 8)
 XRING = 6
 PARTS = 2
 GROUP = 4
-LATER = 3
+LATER = 8
 FSTEP = 5
+ZLATE = 9
 LOADS = 4
 MESH = pl.DeviceIdType.MESH
 
@@ -367,27 +368,27 @@
             transform(x_late, c)
             send_y(1, c + rounds, c, freq)
 
-        @when(t == 1)
+        @when(t == 3)
         def _():
             tables()
 
-        @when((t >= 1) & (t < rounds + 1))
-        def _():
-            collect(1, t - 1)
-
-        @when(t == GROUP)
+        @when((t >= 2) & (t < rounds + 2))
+        def _():
+            collect(1, t - 2)
+
+        @when(t == GROUP + 1)
         def _():
             densify(1, 2, 0)
 
-        @when(t == rounds)
+        @when(t == rounds + 1)
         def _():
             densify(1, 2, 1)
 
-        @when((t >= 3) & (t < rounds + 1))
-        def _():
-            collect(0, t - 3)
-
-        @when(t == GROUP + 2)
+        @when((t >= 4) & (t < rounds + 2))
+        def _():
+            collect(0, t - 4)
+
+        @when(t == GROUP + 3)
         def _():
             densify(0, 0, 0)
 
@@ -400,6 +401,9 @@
             collect(0, rounds - 2)
             collect(0, rounds - 1)
             densify(0, 0, 1)
+
+        @when(t == jnp.where(core == 1, rounds + ZLATE, rounds + 3))
+        def _():
             send_z(0)
 
         @when(t == rounds + FSTEP)
@@ -581,7 +585,7 @@
             dma((2 * LOADS + 5,)),
         ],
         compiler_params=pltpu.CompilerParams(
-            collective_id=0, has_side_effects=True, vmem_limit_bytes=63 * 1024 * 1024),
+            collective_id=0, has_side_effects=True, vmem_limit_bytes=67043328),
     )(cos_weights, pair_occ.T, pair_virt.T, steps,
       both, occupied[0], virtual[0])
 

time: 151 us -> 146 us (0.967)
  Pallas kernels: 145 us -> 139 us
    pallas_call x1, Pallas kernels: 145 us -> 139 us  [body(): pl.pallas_call(functools.partial(main_kernel, ny, nz, groups, terms), out...]
where the time goes in v5:
time: 146 us; the launch traced here: 145 us
  Pallas kernels  139 us (95%)
  local copies, waits for them, and re-layouts  3.95 us (3%)
  other arithmetic  2.29 us (2%)
    pallas_call x1, Pallas kernels, body(): pl.pallas_call(functools.partial(main_kernel, ny, nz, groups, terms), out...  139 us

profile of v5, /device:TPU:1, one launch (start us, length us, event | category | flops | bytes accessed | tf_op | source)
XLA Modules:
  0.0 145.5 jit_solution(9834657789981558339)
XLA Ops:
  0.0 0.1 pad.9.clone
  0.1 0.7 iota_add_fusion.1
  0.8 0.2 convert_reduce_fusion
  1.0 0.3 select_reduce_fusion
  1.3 0.1 fusion.2
  1.4 0.1 convert_reduce_fusion.1
  1.5 0.1 select_reduce_fusion.1
  1.6 0.7 pad_add_fusion.steps_in
  2.3 0.1 sub.32
  2.4 0.1 select_bitcast_fusion.1
  2.5 0.3 copy.10
  2.8 0.1 reshape.107
  3.0 0.3 copy.11
  3.3 0.1 reshape.108
  3.4 0.6 broadcast_in_dim.30.tv_in
  4.0 139.2 %shard_map.64 = f32[4,32,16,128]{3,2,1,0:T(8,128)} custom-call(f32[4,8]{1,0:T(4,128)} %weights_in.1, s32[16,192]{1,0:T(8,128)} %bitcast.11, s32[16,192]{1,0:T(8,128)} %bitcast.12, s32[8,96]{1,0:T(8,128)} %pad_add_fusion.steps_in, s32[8,8,128]{2,1,0:T(8,128)} %broadcast_in_dim.30.tv_in, bf16[128,128,128]{2,1,0:T(8,128)(2,1)} %bitcast.9, ...), custom_call_target="tpu_custom_call" | custom-call | tf_op jit(solution)/shard_map/pallas_call | solution.py:538
  143.2 2.3 %copy.13 = f32[4,32,16,128]{3,2,1,0:T(8,128)} copy(f32[4,32,16,128]{3,2,1,0:T(8,128)} %shard_map.64) | data formatting | bytes 2097152
  (11 shorter events, 0.1 us)

commit v6 on v5

--- a/solution.py
+++ b/solution.py
@@ -15,17 +15,18 @@
 YBUFS = (2, 4)
 RINGS = (6, 8)
 XRING = 6
-PARTS = 2
+PARTS = 6
 GROUP = 4
-LATER = 8
-FSTEP = 5
+LATER = 7
+FSTEP = 7
+ZSOON = 5
 ZLATE = 9
 LOADS = 4
 MESH = pl.DeviceIdType.MESH
 
 
 def main_kernel(ny, nz, groups, terms,
-                weights_in, occ_idx_in, virt_idx_in, steps_in, tv_in, occ_hbm, virt_hbm,
+                weights_in, occ_idx_in, virt_idx_in, tables_in, occ_hbm, virt_hbm,
                 out,
                 occ, virt, weights, occ_idx, virt_idx, steps, tv, early, late, timed, x_early, x_late, freq, y_out_first, y_out_second, y_first, y_second, work, scan, dense, zrecv,
                 final, back, trecv, order_v, spot_v, order, spot,
@@ -73,8 +74,8 @@
     small = [
         pltpu.make_async_copy(source, into, load_sem.at[2 * LOADS + i])
         for i, (source, into) in enumerate((
-            (tv_in, tv), (occ_idx_in, occ_idx), (virt_idx_in, virt_idx),
-            (steps_in, steps), (weights_in, weights)))
+            (tables_in.at[pl.ds(0, 8)], tv), (occ_idx_in, occ_idx), (virt_idx_in, virt_idx),
+            (tables_in.at[8], steps), (weights_in, weights)))
     ]
     for copy in small:
         copy.start()
@@ -133,6 +134,22 @@
             send_sem=z_send.at[(q * 2 + h) * 4 + to],
             recv_sem=z_recv.at[(q * 2 + h) * 4 + source],
             device_id=peer(1 - h, to), device_id_type=MESH)
+
+    def around(h):
+        i, n = mine[1 - h], sizes[1 - h]
+        return i, (i + 1) % n, (i + 2) % n, (i + 3) % n
+
+    def relay_copy(q, h, right, landed):
+        i, after, across, before = around(h)
+        into = i if landed else (after if right else before)
+        mid = CHI_DEV // 2
+        at = pl.ds(0 if right else mid, mid)
+        row = (q * 2 + h) * 4
+        return pltpu.make_async_remote_copy(
+            src_ref=dense.at[q, h, across, at], dst_ref=zrecv.at[q, h, into, at],
+            send_sem=z_send.at[row + (across if right else i)],
+            recv_sem=z_recv.at[row + (into if right else (into + 2) % sizes[1 - h])],
+            device_id=peer(1 - h, after if right else before), device_id_type=MESH)
 
     def back_copy(dest, source):
         return pltpu.make_async_remote_copy(
@@ -298,16 +315,39 @@
             for to in others(1 - h):
                 z_copy(q, h, to, mine[1 - h]).start()
 
+    def send_relay(q):
+        for h in range(2):
+            for right in (True, False):
+                relay_copy(q, h, right, False).start()
+
+    def send_merged(q):
+        for h in range(2):
+            i, after, across, before = around(h)
+            mid = CHI_DEV // 2
+            for right in (True, False):
+                relay_copy(q, h, right, True).wait_recv()
+
+            @pl.loop(0, mid, unroll=4)
+            def _(e):
+                dense[q, h, after, e] += zrecv[q, h, i, e]
+                dense[q, h, before, mid + e] += zrecv[q, h, i, mid + e]
+            z_copy(q, h, after, i).start()
+            z_copy(q, h, before, i).start()
+
+    def givers(q, h):
+        i, after, across, before = around(h)
+        return others(1 - h) if q == 1 else [after, before]
+
     def finish(q, store):
         for h in range(2):
-            for s in others(1 - h):
+            for s in givers(q, h):
                 z_copy(q, h, s, s).wait_recv()
             own = mine[1 - h]
 
             @pl.loop(0, CHI_DEV, unroll=4)
             def _(e):
                 total = dense[q, h, own, e]
-                for s in others(1 - h):
+                for s in givers(q, h):
                     total += zrecv[q, h, s, e]
                 for k in range(half):
                     store(h * half + k, e, total[k])
@@ -394,17 +434,19 @@
 
         @when(t == rounds + 1)
         def _():
-            send_z(2)
+            send_relay(2)
 
         @when(t == rounds + 3)
         def _():
             collect(0, rounds - 2)
             collect(0, rounds - 1)
             densify(0, 0, 1)
-
-        @when(t == jnp.where(core == 1, rounds + ZLATE, rounds + 3))
-        def _():
-            send_z(0)
+            send_relay(0)
+            send_merged(2)
+
+        @when(t == jnp.where(core == 1, rounds + ZLATE, rounds + ZSOON))
+        def _():
+            send_merged(0)
 
         @when(t == rounds + FSTEP)
         def _():
@@ -449,8 +491,11 @@
 
     def drain_z(q):
         for h in range(2):
-            for to in others(1 - h):
+            for to in givers(q, h):
                 z_copy(q, h, to, mine[1 - h]).wait_send()
+            if q != 1:
+                for right in (True, False):
+                    relay_copy(q, h, right, False).wait_send()
 
     def drain_y(q):
         for h in range(2):
@@ -510,7 +555,9 @@
     both = jnp.concatenate([to_y, to_z])
     both = jnp.pad(both, ((0, 0), (0, 128 - both.shape[1])))
     both = jnp.broadcast_to(both[:, None], (both.shape[0], 8, 128))
-    return jnp.concatenate([part, keep, place], axis=1), both
+    steps = jnp.concatenate([part, keep, place], axis=1)
+    steps = jnp.pad(steps, ((0, 0), (0, 128 - steps.shape[1])))
+    return jnp.concatenate([both, steps[None]])
 
 
 def body(occupied, virtual, cos_weights, pair_occ, pair_virt, partial_target_tile):
@@ -531,14 +578,14 @@
     low = rows // 2
     nx = groups // 2
     span = ny * slots * GROUP
-    steps, both = plan(partial_target_tile, owners, ny, nz)
+    both = plan(partial_target_tile, owners, ny, nz)
     vmem = pl.BlockSpec(memory_space=pltpu.VMEM)
     dma = pltpu.SemaphoreType.DMA
     f32 = jnp.float32
     return pl.pallas_call(
         functools.partial(main_kernel, ny, nz, groups, terms),
         out_shape=jax.ShapeDtypeStruct((freqs, CHI_DEV, rows, size), f32),
-        in_specs=[pl.BlockSpec(memory_space=pl.ANY)] * 7,
+        in_specs=[pl.BlockSpec(memory_space=pl.ANY)] * 6,
         out_specs=vmem,
         scratch_shapes=[
             pltpu.VMEM(occupied.shape[1:], occupied.dtype),
@@ -546,8 +593,8 @@
             pltpu.SMEM(cos_weights.shape, f32),
             pltpu.SMEM((terms, count), jnp.int32),
             pltpu.SMEM((terms, count), jnp.int32),
-            pltpu.SMEM(steps.shape, jnp.int32),
-            pltpu.VMEM(both.shape, jnp.int32),
+            pltpu.SMEM(both.shape[1:], jnp.int32),
+            pltpu.VMEM((8,) + both.shape[1:], jnp.int32),
             pltpu.VMEM((PBUFS, groups, per, low, size), f32),
             pltpu.VMEM((CHUNKS, nx, per, low, size), f32),
             pltpu.VMEM((per, nx, low, size), f32),
@@ -586,8 +633,8 @@
         ],
         compiler_params=pltpu.CompilerParams(
             collective_id=0, has_side_effects=True, vmem_limit_bytes=67043328),
-    )(cos_weights, pair_occ.T, pair_virt.T, steps,
-      both, occupied[0], virtual[0])
+    )(cos_weights, pair_occ.T, pair_virt.T, both,
+      occupied[0], virtual[0])
 
 
 def solution(mesh):

time: 146 us -> 142 us (0.973)
  Pallas kernels: 139 us -> 136 us
    pallas_call x1, Pallas kernels: 139 us -> 136 us  [body(): pl.pallas_call(functools.partial(main_kernel, ny, nz, groups, terms), out...]
where the time goes in v6:
time: 142 us; the launch traced here: 141 us
  Pallas kernels  136 us (96%)
  local copies, waits for them, and re-layouts  3.34 us (2%)
  other arithmetic  2.32 us (2%)
    pallas_call x1, Pallas kernels, body(): pl.pallas_call(functools.partial(main_kernel, ny, nz, groups, terms), out...  136 us

profile of v6, /device:TPU:1, one launch (start us, length us, event | category | flops | bytes accessed | tf_op | source)
XLA Modules:
  0.0 141.4 jit_solution(12399574641087185216)
XLA Ops:
  0.0 0.1 pad.13.clone
  0.1 0.7 iota_add_fusion.1
  0.8 0.2 convert_reduce_fusion
  1.0 0.3 select_reduce_fusion
  1.3 0.1 fusion.3
  1.4 0.1 convert_reduce_fusion.1
  1.5 0.1 select_reduce_fusion.1
  1.6 0.1 pad_add_fusion.2
  1.7 0.1 sub.32
  1.9 0.1 select_bitcast_fusion.1
  2.0 0.3 copy.10
  2.3 0.1 reshape.107
  2.4 0.3 copy.11
  2.7 0.1 reshape.108
  2.8 0.6 pad_add_fusion.tables_in
  3.5 135.6 %shard_map.64 = f32[4,32,16,128]{3,2,1,0:T(8,128)} custom-call(f32[4,8]{1,0:T(4,128)} %weights_in.1, s32[16,192]{1,0:T(8,128)} %bitcast.13, s32[16,192]{1,0:T(8,128)} %bitcast.14, s32[9,8,128]{2,1,0:T(8,128)} %pad_add_fusion.tables_in, bf16[128,128,128]{2,1,0:T(8,128)(2,1)} %bitcast.11, bf16[128,128,128]{2,1,0:T(8,128)(2,1)} %bitcast.12), custom_call_target="tpu_custom_call" | custom-call | tf_op jit(solution)/shard_map/pallas_call | solution.py:585
  139.1 2.3 %copy.13 = f32[4,32,16,128]{3,2,1,0:T(8,128)} copy(f32[4,32,16,128]{3,2,1,0:T(8,128)} %shard_map.64) | data formatting | bytes 2097152
  (13 shorter events, 0.1 us)

commit v7 on v6

--- a/solution.py
+++ b/solution.py
@@ -299,21 +299,20 @@
                 scan[r] = value
                 return value
 
-            lax.fori_loop(0, span, one, jnp.zeros((half, low, width), jnp.float32), unroll=8)
+            lax.fori_loop(0, span, one, jnp.zeros((half, low, width), jnp.float32), unroll=16)
 
             @pl.loop(0, sizes[1 - h])
             def _(o):
-                @pl.loop(0, CHI_DEV, unroll=8)
+                @pl.loop(0, CHI_DEV, unroll=16)
                 def _(e):
                     value = scan[spot[at, o * CHI_DEV + e]]
                     if g:
                         value = value + dense[stream, h, o, e]
                     dense[stream, h, o, e] = value
 
-    def send_z(q):
-        for h in range(2):
-            for to in others(1 - h):
-                z_copy(q, h, to, mine[1 - h]).start()
+            if g and stream == 1:
+                for to in others(1 - h):
+                    z_copy(1, h, to, mine[1 - h]).start()
 
     def send_relay(q):
         for h in range(2):
@@ -464,7 +463,6 @@
     @when(core == 1)
     def _():
         densify(1, 1, 1)
-        send_z(1)
 
     finish(0, store_early)
 

time: 142 us -> 141 us (level)
  no operation moved by 1% of the time
where the time goes in v7:
time: 141 us
  Pallas kernels  135 us (96%)
  local copies, waits for them, and re-layouts  3.34 us (2%)
  other arithmetic  2.32 us (2%)
    pallas_call x1, Pallas kernels, body(): pl.pallas_call(functools.partial(main_kernel, ny, nz, groups, terms), out...  135 us

profile of v7, /device:TPU:1, one launch (start us, length us, event | category | flops | bytes accessed | tf_op | source)
XLA Modules:
  0.0 140.9 jit_solution(17767552958439607367)
XLA Ops:
  0.0 0.1 pad.13.clone
  0.1 0.7 iota_add_fusion.1
  0.8 0.2 convert_reduce_fusion
  1.0 0.3 select_reduce_fusion
  1.3 0.1 fusion.3
  1.4 0.1 convert_reduce_fusion.1
  1.5 0.1 select_reduce_fusion.1
  1.6 0.1 pad_add_fusion.2
  1.7 0.1 sub.32
  1.9 0.1 select_bitcast_fusion.1
  2.0 0.3 copy.10
  2.3 0.1 reshape.107
  2.4 0.3 copy.11
  2.7 0.1 reshape.108
  2.8 0.6 pad_add_fusion.tables_in
  3.5 135.2 %shard_map.64 = f32[4,32,16,128]{3,2,1,0:T(8,128)} custom-call(f32[4,8]{1,0:T(4,128)} %weights_in.1, s32[16,192]{1,0:T(8,128)} %bitcast.13, s32[16,192]{1,0:T(8,128)} %bitcast.14, s32[9,8,128]{2,1,0:T(8,128)} %pad_add_fusion.tables_in, bf16[128,128,128]{2,1,0:T(8,128)(2,1)} %bitcast.11, bf16[128,128,128]{2,1,0:T(8,128)(2,1)} %bitcast.12), custom_call_target="tpu_custom_call" | custom-call | tf_op jit(solution)/shard_map/pallas_call | solution.py:583
  138.6 2.3 %copy.13 = f32[4,32,16,128]{3,2,1,0:T(8,128)} copy(f32[4,32,16,128]{3,2,1,0:T(8,128)} %shard_map.64) | data formatting | bytes 2097152
  (13 shorter events, 0.1 us)
